TPU v7x, 128 devices: a whole 4x4x4 slice. The times are simulated.
128 devices in a mesh: seq: 8 (over z_hi, x), exp: 16 (over z_lo, y, core).
Axes of the slice: x: 4, y: 4, z: 4 (z_hi: 2, z_lo: 2; z = z_hi * 2 + z_lo), core: 2. Of those that a mesh axis runs over, the one named last changes fastest.
Arguments:
- queries: bfloat16 [16384, 3072], P(('seq', 'exp')), may hold values from -123 to 123
- keys: bfloat16 [16384, 512], P(('seq', 'exp')), may hold values from -6 to 6
- values: bfloat16 [16384, 512], P(('seq', 'exp')), may hold values from -9 to 9
- residual: bfloat16 [16384, 6144], P(('seq', 'exp')), may hold values from -51 to 51
- proj_weight: bfloat16 [3072, 6144], P('seq', 'exp'), may hold values from -0.109375 to 0.109375
- norm_gain: bfloat16 [6144], replicated, may hold values from 0.099609375 to 1.8984375
- router: bfloat16 [6144, 8], replicated, may hold values from -0.078125 to 0.078125
- expert_ids: int32 [16384, 2], P(('seq', 'exp')), may hold values from 0 to 7, all different within a row; in each aligned block of 128 rows (0 to 127, 128 to 255, ...) at most 33 rows name the same one
- u_gate_up: bfloat16 [16, 3072, 1024], P('exp'), may hold values from -0.078125 to 0.078125
- v_gate_up: bfloat16 [16, 2, 512, 4096], P('exp'), may hold values from -0.25 to 0.25
- u_down: bfloat16 [16, 4096, 512], P('exp'), may hold values from -0.0625 to 0.0625
- v_down: bfloat16 [16, 512, 3072], P('exp'), may hold values from -0.25 to 0.25
Outputs:
- layer_out: bfloat16 [16384, 6144], P(('seq', 'exp'))
Inputs may be any that keep to these rules, and one draw needn't show every extreme that they name: `expert_ids`: the two experts of a token differ. Among the tokens of one device no expert is named more than 33 times, and in some devices' tokens some expert is named exactly 33 times.
All inputs are finite; a program needn't handle non-finite values.
Results may differ from a plain program's by a relative error of at most 0.02.
Values may be sent and summed in bfloat16 or wider, within the bound.
No kernel may reach another device: no remote copies, remote signals or barrier semaphores. Data moves between devices by JAX's collectives and lax.ppermute only.
A program may use at most 192 MiB of HBM per device.

v0:
```python
import functools

import jax
import jax.numpy as jnp
from jax import lax
from jax.experimental import pallas as pl
from jax.experimental.pallas import tpu as pltpu
from jax.sharding import Mesh
from jax.sharding import PartitionSpec as P


D = 6144
HEAD_DIM = 128
GROUP_HEADS = 3
GROUP_WIDTH = GROUP_HEADS * HEAD_DIM
EXPERTS = 8
RANK = 512
FF_PIECE = 4096
TOK_DEV = 128
HALF_TOK = TOK_DEV // 2
HALF = D // 2
BLOCKS = 8
BLOCK_WIDTH = HALF // BLOCKS
SLOTS = 32
PART = 16
EPS = 1e-05
SCALE = HEAD_DIM**-0.5 * 1.4426950408889634
LOW = -1e30
Q_ROWS = 512
Q_TILE = 512
KEY_PART = 256
SOURCES = Q_TILE // HALF_TOK

Z = ("zh", "zl")
PLANE = ("zh", "x", "zl")
GROUP = ("y", "c")
EXP = ("zl", "y", "c")


VMEM = pl.BlockSpec(memory_space=pltpu.VMEM)
SMEM = pl.BlockSpec(memory_space=pltpu.SMEM)
ANY = pl.BlockSpec(memory_space=pl.ANY)
HBM = pl.BlockSpec(memory_space=pltpu.HBM)


def params(mib=48, **more):
    return pltpu.CompilerParams(vmem_limit_bytes=mib << 20, **more)


def cost(flops, moved, transcendentals=0):
    return pl.CostEstimate(flops=flops, bytes_accessed=moved, transcendentals=transcendentals)


def shifted(value, axis, step):
    return lax.ppermute(value, axis, [(i, (i + step) % 4) for i in range(4)])


def other_core(value):
    return lax.ppermute(value, "c", [(0, 1), (1, 0)])


def mirrored(value):
    return lax.ppermute(value, PLANE, [(i, 15 - i) for i in range(16)])


def ring_pieces(value, axis):
    half = value.shape[0] // 2
    up = shifted(value, axis, 1)
    down = shifted(value, axis, -1)
    far_up = shifted(up[:half], axis, 1)
    far_down = shifted(down[half:], axis, -1)
    return [value, up, down, far_up, far_down]


def relative(mine, theirs):
    gap = (mine - theirs) % 4
    return jnp.where(gap == 3, 2, jnp.where(gap == 2, 3, gap))


def direct_pieces(value, axis):
    return [value] + [shifted(value, axis, step) for step in (1, -1, 2)]


def pack_kernel(*refs):
    sources, out_ref, sems = refs[:-2], refs[-2], refs[-1]
    count, width = out_ref.shape[0], out_ref.shape[2] // len(sources)
    copies = []
    for place in range(count):
        for number, source in enumerate(sources):
            copies.append(
                pltpu.make_async_copy(
                    source.at[:, pl.ds(place * width, width)],
                    out_ref.at[place, :, pl.ds(number * width, width)],
                    sems.at[place * len(sources) + number],
                )
            )
    for copy in copies:
        copy.start()
    for copy in copies:
        copy.wait()


def packed(sources, shape):
    return pl.pallas_call(
        pack_kernel,
        out_shape=jax.ShapeDtypeStruct(shape, jnp.bfloat16),
        in_specs=[ANY] * len(sources),
        out_specs=VMEM,
        scratch_shapes=[pltpu.SemaphoreType.DMA((shape[0] * len(sources),))],
        compiler_params=params(8),
        cost_estimate=cost(1_000_000_000, 2_000_000),
        name="pack",
    )(*sources)


def pack_kv(keys, values):
    return packed((keys, values), (4, TOK_DEV, 2 * HEAD_DIM))


def pack_q_kernel(near_ref, far_ref, out_ref, sems):
    copies = []
    for place in range(8):
        columns = pl.ds(place * GROUP_WIDTH, GROUP_WIDTH)
        for slot, source in enumerate((near_ref, far_ref)):
            copies.append(
                pltpu.make_async_copy(
                    source.at[pl.ds(0, HALF_TOK), columns],
                    out_ref.at[place, pl.ds(slot * HALF_TOK, HALF_TOK), :],
                    sems.at[place * 2 + slot],
                )
            )
    for copy in copies:
        copy.start()
    for copy in copies:
        copy.wait()


def pack_q(queries, far):
    return pl.pallas_call(
        pack_q_kernel,
        out_shape=jax.ShapeDtypeStruct((8, TOK_DEV, GROUP_WIDTH), jnp.bfloat16),
        in_specs=[ANY, ANY],
        out_specs=VMEM,
        scratch_shapes=[pltpu.SemaphoreType.DMA((16,))],
        compiler_params=params(8),
        cost_estimate=cost(1_000_000_000, 2_000_000),
        name="pack_q",
    )(queries, far)


def attention_kernel(items, kpos_ref, q_ref, *refs):
    pieces = refs[:20]
    out_ref = refs[20]
    kv_ref, max_ref, acc_ref, sems = refs[21:]
    copies = []
    for which in range(4):
        for number in range(5):
            source = pieces[which * 5 + number]
            if number < 3:
                target = kv_ref.at[which, pl.ds(number * 4, 4)]
            else:
                target = kv_ref.at[which, pl.ds(12 + (number - 3) * 2, 2)]
            copies.append(pltpu.make_async_copy(source, target, sems.at[which * 5 + number]))
    for copy in copies:
        copy.start()
    max_ref[...] = jnp.full(max_ref.shape, LOW, jnp.float32)
    acc_ref[...] = jnp.zeros(acc_ref.shape, jnp.float32)
    for copy in copies:
        copy.wait()

    def load(at):
        keys, values = [], []
        ones = jnp.ones((KEY_PART, HEAD_DIM), jnp.bfloat16)
        for which in range(4):
            block = at[which % 2]
            keys.append(kv_ref[which, block, :, 0:HEAD_DIM])
            value = kv_ref[which, block, :, HEAD_DIM : 2 * HEAD_DIM]
            values.append(jnp.concatenate([value, ones], axis=1))
        return keys, values

    def score(slot, keys, tile, head):
        low = head * HEAD_DIM
        lanes = pl.ds(low if isinstance(low, int) else pl.multiple_of(low, HEAD_DIM), HEAD_DIM)
        query = q_ref[
            pl.ds(tile * SOURCES, SOURCES),
            pl.ds(pl.multiple_of(slot * HALF_TOK, HALF_TOK), HALF_TOK),
            lanes,
        ].reshape(Q_TILE, HEAD_DIM)
        return [
            lax.dot_general(
                query, key, (((1,), (1,)), ((), ())), preferred_element_type=jnp.float32
            )
            for key in keys
        ]

    def absorb(slot, values, tile, head, scores):
        rows = pl.ds(tile * Q_TILE, Q_TILE)
        highest = jnp.maximum(
            jnp.maximum(scores[0], scores[1]), jnp.maximum(scores[2], scores[3])
        )
        old_max = max_ref[slot, head, rows, :]
        new_max = jnp.maximum(old_max, jnp.max(highest, axis=1, keepdims=True))
        level = jnp.tile(new_max * SCALE, (1, KEY_PART // HEAD_DIM))
        update = None
        for which in range(4):
            weights = jnp.exp2(scores[which] * SCALE - level).astype(jnp.bfloat16)
            term = jnp.dot(weights, values[which], preferred_element_type=jnp.float32)
            update = term if update is None else update + term
        fading = jnp.exp2((old_max - new_max) * SCALE)
        max_ref[slot, head, rows, :] = new_max
        acc_ref[slot, head, rows, 0:HEAD_DIM] = (
            acc_ref[slot, head, rows, 0:HEAD_DIM] * fading + update[:, :HEAD_DIM]
        )
        acc_ref[slot, head, rows, HEAD_DIM:] = (
            acc_ref[slot, head, rows, HEAD_DIM:] * fading + update[:, HEAD_DIM:]
        )

    def work(slot, at, masked):
        keys, values = load(at)
        if masked:

            def masked_head(head, carry):
                for tile in range(Q_ROWS // Q_TILE):
                    scores = score(slot, keys, tile, head)
                    row = lax.broadcasted_iota(jnp.int32, (Q_TILE, KEY_PART), 0)
                    row_pos = (
                        (tile * SOURCES + row // HALF_TOK) * TOK_DEV
                        + slot * HALF_TOK
                        + row % HALF_TOK
                    )
                    scores = [
                        jnp.where(kpos_ref[which : which + 1, :] <= row_pos, part, LOW)
                        for which, part in enumerate(scores)
                    ]
                    absorb(slot, values, tile, head, scores)
                return carry

            lax.fori_loop(0, GROUP_HEADS, masked_head, 0)
            return
        steps = [(t, h) for t in range(Q_ROWS // Q_TILE) for h in range(GROUP_HEADS)]
        waiting = score(slot, keys, *steps[0])
        for number, (tile, head) in enumerate(steps):
            ready = waiting
            if number + 1 < len(steps):
                waiting = score(slot, keys, *steps[number + 1])
            absorb(slot, values, tile, head, ready)

    open_count = items[0]
    masked_count = items[1]

    def open_step(number, carry):
        at = 2 + 3 * number
        work(items[at], (items[at + 1], items[at + 2]), False)
        return carry

    def masked_step(number, carry):
        at = 2 + 3 * (open_count + number)
        work(items[at], (items[at + 1], items[at + 2]), True)
        return carry

    lax.fori_loop(0, open_count, open_step, 0)
    lax.fori_loop(0, masked_count, masked_step, 0)
    for slot in range(2):
        for head in range(GROUP_HEADS):
            out_ref[slot, :, head * HEAD_DIM : (head + 1) * HEAD_DIM] = (
                acc_ref[slot, head, :, 0:HEAD_DIM] / acc_ref[slot, head, :, HEAD_DIM:]
            ).astype(jnp.bfloat16)


def attention(items, kpos, query_pair, pieces):
    shaped = [p.reshape(-1, KEY_PART, 2 * HEAD_DIM) for p in pieces]
    return pl.pallas_call(
        attention_kernel,
        out_shape=jax.ShapeDtypeStruct((2, Q_ROWS, GROUP_WIDTH), jnp.bfloat16),
        in_specs=[SMEM, VMEM, VMEM] + [ANY] * 20,
        out_specs=VMEM,
        scratch_shapes=[
            pltpu.VMEM((4, 16, KEY_PART, 2 * HEAD_DIM), jnp.bfloat16),
            pltpu.VMEM((2, GROUP_HEADS, Q_ROWS, HEAD_DIM), jnp.float32),
            pltpu.VMEM((2, GROUP_HEADS, Q_ROWS, 2 * HEAD_DIM), jnp.float32),
            pltpu.SemaphoreType.DMA((20,)),
        ],
        compiler_params=params(28),
        cost_estimate=cost(27_000_000_000, 10_000_000, 26_000_000),
        name="attention",
    )(items, kpos, query_pair, *shaped)


def projection_kernel(first, groups, w_ref, *refs):
    pieces = refs[:10]
    if first:
        w_all = w_ref
        out_ref, rows_ref, done_ref, sems, w_sems, out_sem = refs[-6:]
    else:
        out_ref, w_all, rows_ref, done_ref, sems, w_sems, out_sem = refs[-7:]
    copies = []
    for core in range(2):
        for number in range(4):
            at = (core * 4 + number) * GROUP_WIDTH
            for side in range(0 if first else 2):
                copies.append(
                    pltpu.make_async_copy(
                        w_ref.at[groups[core * 4 + number], side],
                        w_all.at[pl.ds(at, GROUP_WIDTH), pl.ds(side * GROUP_WIDTH, GROUP_WIDTH)],
                        w_sems.at[(core * 4 + number) * 2 + side],
                    )
                )
        for number in range(5):
            at = (core * 4 + min(number, 3)) * GROUP_WIDTH
            source = pieces[core * 5 + number]
            low = 256 if number == 4 else 0
            copies.append(
                pltpu.make_async_copy(
                    source,
                    rows_ref.at[pl.ds(low, source.shape[0]), pl.ds(at, GROUP_WIDTH)],
                    sems.at[core * 5 + number],
                )
            )
    for copy in copies:
        copy.start()
    for copy in copies:
        copy.wait()
    for tile in range(Q_ROWS // Q_TILE):
        total = jnp.dot(
            rows_ref[tile * Q_TILE : (tile + 1) * Q_TILE, :],
            w_all[...],
            preferred_element_type=jnp.float32,
        )
        done_ref[tile * SOURCES : (tile + 1) * SOURCES] = total.astype(jnp.bfloat16).reshape(
            SOURCES, HALF_TOK, 2 * GROUP_WIDTH
        )
    out = pltpu.make_async_copy(done_ref, out_ref.at[:, pl.ds(first, HALF_TOK), :], out_sem)
    out.start()
    out.wait()


def projection(first, groups, weights, pieces, before):
    more = [] if before is None else [before]
    out = jax.ShapeDtypeStruct((8, TOK_DEV, 2 * GROUP_WIDTH), jnp.bfloat16)
    arranged = jax.ShapeDtypeStruct((8 * GROUP_WIDTH, 2 * GROUP_WIDTH), jnp.bfloat16)
    return pl.pallas_call(
        functools.partial(projection_kernel, first),
        out_shape=out if more else (out, arranged),
        in_specs=[SMEM] + [VMEM if more else ANY] + [ANY] * (10 + len(more)),
        out_specs=HBM if more else (HBM, VMEM),
        scratch_shapes=[
            pltpu.VMEM((Q_ROWS, 8 * GROUP_WIDTH), jnp.bfloat16),
            pltpu.VMEM((8, HALF_TOK, 2 * GROUP_WIDTH), jnp.bfloat16),
            pltpu.SemaphoreType.DMA((10,)),
            pltpu.SemaphoreType.DMA((16,)),
            pltpu.SemaphoreType.DMA,
        ],
        input_output_aliases={12: 0} if more else {},
        compiler_params=params(16),
        cost_estimate=cost(2_500_000_000, 9_000_000),
        name="projection",
    )(groups, weights, *pieces, *more)


def slot_tables(ids_t):
    expert = lax.broadcasted_iota(jnp.int32, (EXPERTS, TOK_DEV), 0)
    first = (expert == ids_t[0:1, :]).astype(jnp.float32)
    second = (expert == ids_t[1:2, :]).astype(jnp.float32)
    member = first + second
    before = (
        lax.broadcasted_iota(jnp.int32, (TOK_DEV, TOK_DEV), 0)
        < lax.broadcasted_iota(jnp.int32, (TOK_DEV, TOK_DEV), 1)
    ).astype(jnp.bfloat16)
    slot = jnp.dot(member.astype(jnp.bfloat16), before, preferred_element_type=jnp.float32)
    return first, second, member, slot


def dispatch_kernel(ids_ref, update_ref, residual_ref, gain_ref, router_ref, send_ref, mix_ref, normed_ref):
    squares = jnp.zeros((TOK_DEV, 1), jnp.float32)
    for half in range(2):
        for group in range(BLOCKS):
            at = half * HALF + group * BLOCK_WIDTH
            row = residual_ref[:, at : at + BLOCK_WIDTH].astype(jnp.float32) + update_ref[
                group, :, half * BLOCK_WIDTH : (half + 1) * BLOCK_WIDTH
            ].astype(jnp.float32)
            squares = squares + jnp.sum(row * row, axis=1, keepdims=True)
    factor = lax.rsqrt(squares / D + EPS)
    for half in range(2):
        for group in range(BLOCKS):
            at = half * HALF + group * BLOCK_WIDTH
            row = residual_ref[:, at : at + BLOCK_WIDTH].astype(jnp.float32) + update_ref[
                group, :, half * BLOCK_WIDTH : (half + 1) * BLOCK_WIDTH
            ].astype(jnp.float32)
            gain = gain_ref[:, at : at + BLOCK_WIDTH].astype(jnp.float32)
            normed_ref[:, at : at + BLOCK_WIDTH] = (row * factor * gain).astype(jnp.bfloat16)
    first, second, member, slot = slot_tables(ids_ref[...])
    slot_ids = lax.broadcasted_iota(jnp.int32, (SLOTS, TOK_DEV), 0).astype(jnp.float32)
    picks, tails = [], []
    last = jnp.where(slot == float(SLOTS), member, 0.0)
    for expert in range(EXPERTS):
        picks.append(
            jnp.where(slot[expert : expert + 1, :] == slot_ids, member[expert : expert + 1, :], 0.0)
        )
        tails.append(jnp.broadcast_to(last[expert : expert + 1, :], (BLOCKS, TOK_DEV)))
    pick = jnp.concatenate(picks, axis=0)
    tail = jnp.concatenate(tails, axis=0)
    tail_block = lax.broadcasted_iota(jnp.int32, (EXPERTS * BLOCKS, TOK_DEV), 0) % BLOCKS
    pick_low = pick.astype(jnp.bfloat16)
    for half in range(2):

        def one_block(block, tail_rows):
            at = pl.multiple_of(half * HALF + block * BLOCK_WIDTH, BLOCK_WIDTH)
            rows = normed_ref[:, pl.ds(at, BLOCK_WIDTH)]
            moved = jnp.dot(pick_low, rows, preferred_element_type=jnp.float32).astype(jnp.bfloat16)
            place = pl.ds(pl.multiple_of(block * SLOTS, SLOTS), SLOTS)
            for expert in range(EXPERTS):
                send_ref[2 * expert + half, place, :] = moved[
                    expert * SLOTS : (expert + 1) * SLOTS, :
                ]
            chosen = jnp.where(tail_block == block, tail, 0.0).astype(jnp.bfloat16)
            return tail_rows + jnp.dot(chosen, rows, preferred_element_type=jnp.float32)

        empty = jnp.zeros((EXPERTS * BLOCKS, BLOCK_WIDTH), jnp.float32)
        tail_rows = lax.fori_loop(0, BLOCKS, one_block, empty)
        tail_rows = tail_rows.astype(jnp.bfloat16)
        for expert in range(EXPERTS):
            send_ref[2 * expert + half, BLOCKS * SLOTS :, :] = tail_rows[
                expert * BLOCKS : (expert + 1) * BLOCKS, :
            ]
    logits = lax.dot_general(
        router_ref[...],
        normed_ref[...],
        (((1,), (1,)), ((), ())),
        preferred_element_type=jnp.float32,
    )
    chosen_first = jnp.sum(first * logits, axis=0, keepdims=True)
    chosen_second = jnp.sum(second * logits, axis=0, keepdims=True)
    mix_first = 1.0 / (1.0 + jnp.exp(chosen_second - chosen_first))
    mix_second = 1.0 / (1.0 + jnp.exp(chosen_first - chosen_second))
    share = first * mix_first + second * mix_second
    for expert in range(EXPERTS):
        mine = share[expert : expert + 1, :]
        mix_ref[expert * SLOTS : (expert + 1) * SLOTS, :] = picks[expert] * mine
        mix_ref[
            EXPERTS * SLOTS + expert * BLOCKS : EXPERTS * SLOTS + (expert + 1) * BLOCKS, :
        ] = tails[expert] * mine


def dispatch(ids_t, update, residual, gain, router_t):
    return pl.pallas_call(
        dispatch_kernel,
        out_shape=(
            jax.ShapeDtypeStruct((16, BLOCKS * (SLOTS + 1), BLOCK_WIDTH), jnp.bfloat16),
            jax.ShapeDtypeStruct((EXPERTS * (SLOTS + BLOCKS), TOK_DEV), jnp.float32),
        ),
        in_specs=[VMEM] * 5,
        out_specs=(VMEM, VMEM),
        scratch_shapes=[pltpu.VMEM((TOK_DEV, D), jnp.bfloat16)],
        compiler_params=params(32),
        cost_estimate=cost(800_000_000, 8_000_000),
        name="dispatch",
    )(ids_t, update, residual, gain, router_t)


PARTS = SLOTS // PART
ROWS = 16 * SLOTS
ALL_ROWS = ROWS + 16
GROUPS = 4
GROUP_DEPTH = HALF // GROUPS


def row_pick(block):
    source = lax.broadcasted_iota(jnp.int32, (16, 16 * BLOCKS), 0)
    place = lax.broadcasted_iota(jnp.int32, (16, 16 * BLOCKS), 1)
    return (place == source * BLOCKS + block).astype(jnp.bfloat16)


def first_kernel(rows_ref, u_ref, low_ref, x_ref, tail_ref, w_ref, acc_ref, sems, row_sems):
    copies = []
    for group in range(GROUPS):
        rows = pl.ds(group * GROUP_DEPTH, GROUP_DEPTH)
        copies.append(pltpu.make_async_copy(u_ref.at[0, rows], w_ref.at[rows], sems.at[group]))
    moves = [
        pltpu.make_async_copy(
            rows_ref.at[:, pl.ds(BLOCKS * SLOTS, BLOCKS), :], tail_ref, row_sems.at[2 * BLOCKS]
        )
    ]
    for block in range(BLOCKS):
        for part in range(PARTS):
            moves.append(
                pltpu.make_async_copy(
                    rows_ref.at[:, pl.ds(block * SLOTS + part * PART, PART), :],
                    x_ref.at[pl.ds(part * 16, 16), :, pl.ds(block * BLOCK_WIDTH, BLOCK_WIDTH)],
                    row_sems.at[block * PARTS + part],
                )
            )
    for move in moves[: 1 + 2 * PARTS]:
        move.start()
    copies[0].start()
    for move in moves[1 + 2 * PARTS :]:
        move.start()
    for copy in copies[1:]:
        copy.start()
    moves[0].wait()
    tail = tail_ref[...].reshape(16 * BLOCKS, BLOCK_WIDTH)
    for block in range(BLOCKS):
        picked = jnp.dot(row_pick(block), tail, preferred_element_type=jnp.float32)
        x_ref[2 * 16, :, block * BLOCK_WIDTH : (block + 1) * BLOCK_WIDTH] = picked.astype(
            jnp.bfloat16
        )
    each = BLOCKS // GROUPS * PARTS
    for group in range(GROUPS):
        at = group * GROUP_DEPTH
        for move in moves[1 + group * each : 1 + (group + 1) * each]:
            move.wait()
        copies[group].wait()
        rows = x_ref[:, :, at : at + GROUP_DEPTH].reshape(ALL_ROWS, GROUP_DEPTH)
        term = jnp.dot(rows, w_ref[at : at + GROUP_DEPTH, :], preferred_element_type=jnp.float32)
        if group == 0:
            acc_ref[...] = term
        elif group < GROUPS - 1:
            acc_ref[...] += term
        else:
            low_ref[...] = (acc_ref[...] + term).astype(jnp.bfloat16)


def first_factor(received, u_gate_up):
    return pl.pallas_call(
        first_kernel,
        out_shape=jax.ShapeDtypeStruct((ALL_ROWS, 2 * RANK), jnp.bfloat16),
        in_specs=[ANY, ANY],
        out_specs=VMEM,
        scratch_shapes=[
            pltpu.VMEM((16 * PARTS + 1, PART, HALF), jnp.bfloat16),
            pltpu.VMEM((16, BLOCKS, BLOCK_WIDTH), jnp.bfloat16),
            pltpu.VMEM((HALF, 2 * RANK), jnp.bfloat16),
            pltpu.VMEM((ALL_ROWS, 2 * RANK), jnp.float32),
            pltpu.SemaphoreType.DMA((GROUPS,)),
            pltpu.SemaphoreType.DMA((BLOCKS * PARTS + 1,)),
        ],
        compiler_params=params(58),
        cost_estimate=cost(3_400_000_000, 9_000_000),
        name="first_factor",
    )(received, u_gate_up)


FF_TILE = 512
FF_STEPS = FF_PIECE // FF_TILE


def middle_kernel(own_ref, got_ref, v_ref, u_ref, low_ref, rank_ref, vs_ref, us_ref, acc_ref, sems):
    copies = []
    for step in range(FF_STEPS):
        columns = pl.ds(step * FF_TILE, FF_TILE)
        copies.append(
            (
                pltpu.make_async_copy(
                    v_ref.at[0, :, :, columns], vs_ref.at[:, :, columns], sems.at[2 * step]
                ),
                pltpu.make_async_copy(
                    u_ref.at[0, columns, :], us_ref.at[columns, :], sems.at[2 * step + 1]
                ),
            )
        )
    for pair in copies:
        for copy in pair:
            copy.start()
    rank_ref[...] = (
        own_ref[...].astype(jnp.float32) + got_ref[...].astype(jnp.float32)
    ).astype(jnp.bfloat16)
    acc_ref[...] = jnp.zeros(acc_ref.shape, jnp.float32)

    def one_tile(step, carry):
        columns = pl.ds(pl.multiple_of(step * FF_TILE, FF_TILE), FF_TILE)
        pltpu.make_async_copy(
            v_ref.at[0, :, :, columns], vs_ref.at[:, :, columns], sems.at[2 * step]
        ).wait()
        pltpu.make_async_copy(
            u_ref.at[0, columns, :], us_ref.at[columns, :], sems.at[2 * step + 1]
        ).wait()
        gate = jnp.dot(rank_ref[:, :RANK], vs_ref[0, :, columns], preferred_element_type=jnp.float32)
        up = jnp.dot(rank_ref[:, RANK:], vs_ref[1, :, columns], preferred_element_type=jnp.float32)
        low = 0.5 * gate
        hidden = ((low + low * jnp.tanh(low)) * up).astype(jnp.bfloat16)
        acc_ref[...] += jnp.dot(hidden, us_ref[columns, :], preferred_element_type=jnp.float32)
        return carry

    lax.fori_loop(0, FF_STEPS, one_tile, 0)
    low_ref[...] = acc_ref[...].astype(jnp.bfloat16)


def middle(own, got, v_gate_up, u_down):
    return pl.pallas_call(
        middle_kernel,
        out_shape=jax.ShapeDtypeStruct((ALL_ROWS, RANK), jnp.bfloat16),
        in_specs=[VMEM, VMEM, ANY, ANY],
        out_specs=VMEM,
        scratch_shapes=[
            pltpu.VMEM((ALL_ROWS, 2 * RANK), jnp.bfloat16),
            pltpu.VMEM((2, RANK, FF_PIECE), jnp.bfloat16),
            pltpu.VMEM((FF_PIECE, RANK), jnp.bfloat16),
            pltpu.VMEM((ALL_ROWS, RANK), jnp.float32),
            pltpu.SemaphoreType.DMA((2 * FF_STEPS,)),
        ],
        compiler_params=params(60),
        cost_estimate=cost(6_700_000_000, 14_000_000, 2_200_000),
        name="middle",
    )(own, got, v_gate_up, u_down)


def last_kernel(own_ref, got_ref, v_ref, out_ref, down_ref, w_ref, tail_ref, sems):
    copies = []
    for block in range(BLOCKS):
        columns = pl.ds(block * BLOCK_WIDTH, BLOCK_WIDTH)
        copies.append(
            pltpu.make_async_copy(v_ref.at[0, :, columns], w_ref.at[:, columns], sems.at[block])
        )
    for copy in copies:
        copy.start()
    down_ref[...] = (
        own_ref[...].astype(jnp.float32) + got_ref[...].astype(jnp.float32)
    ).astype(jnp.bfloat16)
    place = lax.broadcasted_iota(jnp.int32, (16 * BLOCKS, 16), 0)
    source = lax.broadcasted_iota(jnp.int32, (16 * BLOCKS, 16), 1)
    tail_ref[...] = jnp.zeros(tail_ref.shape, jnp.float32)

    def one_block(block, carry):
        columns = pl.ds(pl.multiple_of(block * BLOCK_WIDTH, BLOCK_WIDTH), BLOCK_WIDTH)
        pltpu.make_async_copy(v_ref.at[0, :, columns], w_ref.at[:, columns], sems.at[block]).wait()
        spread = (place == source * BLOCKS + block).astype(jnp.bfloat16)
        lifted = jnp.dot(spread, down_ref[ROWS:, :], preferred_element_type=jnp.float32)
        rows = jnp.concatenate([down_ref[:ROWS, :], lifted.astype(jnp.bfloat16)], axis=0)
        result = jnp.dot(rows, w_ref[:, columns], preferred_element_type=jnp.float32)
        main = result[:ROWS].astype(jnp.bfloat16).reshape(PARTS, 16, PART, BLOCK_WIDTH)
        for part in range(PARTS):
            at = pl.ds(pl.multiple_of(block * SLOTS + part * PART, PART), PART)
            out_ref[:, at, :] = main[part]
        tail_ref[...] += result[ROWS:]
        return carry

    lax.fori_loop(0, BLOCKS, one_block, 0)
    out_ref[:, BLOCKS * SLOTS :, :] = (
        tail_ref[...].astype(jnp.bfloat16).reshape(16, BLOCKS, BLOCK_WIDTH)
    )


def last_factor(own, got, v_down):
    return pl.pallas_call(
        last_kernel,
        out_shape=jax.ShapeDtypeStruct((16, BLOCKS * (SLOTS + 1), BLOCK_WIDTH), jnp.bfloat16),
        in_specs=[VMEM, VMEM, ANY],
        out_specs=VMEM,
        scratch_shapes=[
            pltpu.VMEM((ALL_ROWS, RANK), jnp.bfloat16),
            pltpu.VMEM((RANK, HALF), jnp.bfloat16),
            pltpu.VMEM((16 * BLOCKS, BLOCK_WIDTH), jnp.float32),
            pltpu.SemaphoreType.DMA((BLOCKS,)),
        ],
        compiler_params=params(24),
        cost_estimate=cost(1_700_000_000, 6_000_000),
        name="last_factor",
    )(own, got, v_down)


def combine_kernel(mix_ref, update_ref, residual_ref, back_ref, out_ref):
    mix = mix_ref[: EXPERTS * SLOTS, :].T
    tail = mix_ref[EXPERTS * SLOTS :, :].T
    mix_high = mix.astype(jnp.bfloat16)
    mix_low = (mix - mix_high.astype(jnp.float32)).astype(jnp.bfloat16)
    tail_block = lax.broadcasted_iota(jnp.int32, (TOK_DEV, EXPERTS * BLOCKS), 1) % BLOCKS
    for half in range(2):
        tail_rows = jnp.concatenate(
            [back_ref[2 * expert + half, BLOCKS * SLOTS :, :] for expert in range(EXPERTS)], axis=0
        )

        def one_block(block, carry):
            at_rows = pl.ds(pl.multiple_of(block * SLOTS, SLOTS), SLOTS)
            rows = jnp.concatenate(
                [back_ref[2 * expert + half, at_rows, :] for expert in range(EXPERTS)], axis=0
            )
            here = jnp.where(tail_block == block, tail, 0.0)
            here_high = here.astype(jnp.bfloat16)
            here_low = (here - here_high.astype(jnp.float32)).astype(jnp.bfloat16)
            mixture = jnp.dot(mix_high, rows, preferred_element_type=jnp.float32)
            mixture = mixture + jnp.dot(mix_low, rows, preferred_element_type=jnp.float32)
            mixture = mixture + jnp.dot(here_high, tail_rows, preferred_element_type=jnp.float32)
            mixture = mixture + jnp.dot(here_low, tail_rows, preferred_element_type=jnp.float32)
            at = pl.ds(pl.multiple_of(half * HALF + block * BLOCK_WIDTH, BLOCK_WIDTH), BLOCK_WIDTH)
            stream = residual_ref[:, at].astype(jnp.float32) + update_ref[
                block, :, half * BLOCK_WIDTH : (half + 1) * BLOCK_WIDTH
            ].astype(jnp.float32)
            out_ref[:, at] = (stream + mixture).astype(jnp.bfloat16)
            return carry

        lax.fori_loop(0, BLOCKS, one_block, 0)


def combine(mix, update, residual, back):
    return pl.pallas_call(
        combine_kernel,
        out_shape=jax.ShapeDtypeStruct((TOK_DEV, D), jnp.bfloat16),
        in_specs=[VMEM] * 4,
        out_specs=VMEM,
        compiler_params=params(32),
        cost_estimate=cost(1_000_000_000, 8_000_000),
        name="combine",
    )(mix, update, residual, back)


def per_device(
    queries,
    keys,
    values,
    residual,
    proj_weight,
    norm_gain,
    router,
    expert_ids,
    u_gate_up,
    v_gate_up,
    u_down,
    v_down,
):
    zh, x, zl = lax.axis_index("zh"), lax.axis_index("x"), lax.axis_index("zl")
    y, c = lax.axis_index("y"), lax.axis_index("c")
    z = zh * 2 + zl
    chunk = zh * 8 + x * 2 + zl

    q_far = mirrored(queries[HALF_TOK:])
    kv = pack_kv(keys, values)
    kv = lax.all_to_all(kv, "y", split_axis=0, concat_axis=0, tiled=True)
    kv = kv.reshape(4 * TOK_DEV, 2 * HEAD_DIM)
    early, late = kv[:256], kv[256:]

    copies = jnp.broadcast_to(proj_weight[None], (16, GROUP_WIDTH, GROUP_WIDTH))
    q = pack_q(queries, q_far)
    q = lax.all_to_all(q, GROUP, split_axis=0, concat_axis=0, tiled=True)

    def joined(pieces):
        return jnp.concatenate(pieces, axis=0)

    early = joined(direct_pieces(early, Z))
    late = joined(direct_pieces(late, "x"))
    own = ring_pieces(early, "x") + ring_pieces(late, Z)
    swapped = [other_core(p) for p in own]

    far_chunk = 15 - chunk
    order = jnp.arange(15, dtype=jnp.int32)
    is_far = order >= chunk
    slot_list = jnp.concatenate([is_far.astype(jnp.int32), jnp.array([0, 1], jnp.int32)])
    chunk_list = jnp.concatenate(
        [jnp.where(is_far, order - chunk, order), jnp.stack([chunk, far_chunk])]
    )
    there_z = chunk_list // 8 * 2 + chunk_list % 2
    there_x = chunk_list // 2 % 4
    rel_z = relative(z, there_z)
    rel_x = relative(x, there_x)
    rows = jnp.stack([slot_list, rel_x * 4 + rel_z, rel_z * 4 + rel_x], axis=1)
    items = jnp.concatenate([jnp.array([15, 2], jnp.int32), rows.reshape(-1)]).astype(jnp.int32)
    key_ids = jnp.arange(KEY_PART, dtype=jnp.int32)
    base = key_ids // TOK_DEV * 256 + key_ids % TOK_DEV
    kpos = jnp.stack(
        [
            base + c * TOK_DEV,
            base + c * TOK_DEV + 512,
            base + (1 - c) * TOK_DEV,
            base + (1 - c) * TOK_DEV + 512,
        ]
    ).astype(jnp.int32)

    attended = attention(items, kpos, q, own + swapped)
    weight_rows = lax.all_to_all(copies, PLANE, split_axis=0, concat_axis=0, tiled=True)
    weight_rows = weight_rows.reshape(8, 2, GROUP_WIDTH, GROUP_WIDTH)
    from_y = jnp.stack([y, (y - 1) % 4, (y + 1) % 4, (y + 2) % 4])
    groups = jnp.concatenate([from_y * 2 + c, from_y * 2 + 1 - c]).astype(jnp.int32)
    near = ring_pieces(attended[0], "y")
    far = mirrored(attended[1])
    near = near + [other_core(p) for p in near]
    far = ring_pieces(far, "y")
    far = far + [other_core(p) for p in far]
    projected, arranged = projection(0, groups, weight_rows, near, None)
    projected = projection(HALF_TOK, groups, arranged, far, projected)
    update = lax.all_to_all(projected, GROUP, split_axis=0, concat_axis=0, tiled=True)

    ids_t = expert_ids.T
    send, mix = dispatch(ids_t, update, residual, norm_gain.reshape(1, D), router.T)
    received = lax.all_to_all(send, EXP, split_axis=0, concat_axis=0, tiled=True)
    rank_low = first_factor(received, u_gate_up)
    down_low = middle(rank_low, other_core(rank_low), v_gate_up, u_down)
    out_rows = last_factor(down_low, other_core(down_low), v_down)
    back = lax.all_to_all(out_rows, EXP, split_axis=0, concat_axis=0, tiled=True)
    return combine(mix, update, residual, back)


def solution(mesh):
    fine = Mesh(mesh.devices.reshape(2, 4, 2, 4, 2), ("zh", "x", "zl", "y", "c"))
    seq, exp = ("zh", "x"), ("zl", "y", "c")
    in_specs = (
        P(seq + exp, None),
        P(seq + exp, None),
        P(seq + exp, None),
        P(seq + exp, None),
        P(seq, exp),
        P(),
        P(),
        P(seq + exp, None),
        P(exp, None, None),
        P(exp, None, None, None),
        P(exp, None, None),
        P(exp, None, None),
    )

    return jax.shard_map(
        per_device, mesh=fine, in_specs=in_specs, out_specs=P(seq + exp, None), check_vma=False
    )
```

profile of v0, /device:TPU:8, one launch (start us, length us, event | category | flops | bytes accessed | tf_op | source)
XLA Modules:
  0.0 349.5 jit_solution(10511547266675978956)
XLA Ops:
  2.0 9.9 %all_to_all.30 = bf16[4,128,256]{2,1,0:T(8,128)(2,1)S(1)} all-to-all(bf16[4,128,256]{2,1,0:T(8,128)(2,1)S(1)} %pack.1), channel_id=1, replica_groups=mesh['zh'=2,'x'=4,'zl'=2,'y'=4,'c'=2] {'y'}, dimensions={0} | all-to-all | bytes 524288 | tf_op jit(solution)/shard_map/all_to_all | solution.py:726
  31.3 9.7 %collective-permute-done.10 = bf16[256,256]{1,0:T(8,128)(2,1)S(1)} collective-permute-done((bf16[256,256]{1,0:T(8,128)(2,1)S(1)}, bf16[256,256]{1,0:T(8,128)(2,1)S(1)}, u32[]{:S(2)}, u32[]{:S(2)}) %collective-permute-start.10) | collective-permute-done | bytes 131104 | tf_op jit(solution)/shard_map/ppermute | solution.py:55
  48.2 5.5 %collective-permute-done.far_ref = bf16[64,3072]{1,0:T(8,128)(2,1)} collective-permute-done((bf16[64,3072]{1,0:T(8,128)(2,1)}, bf16[64,3072]{1,0:T(8,128)(2,1)}, u32[]{:S(2)}, u32[]{:S(2)}) %collective-permute-start) | collective-permute-done | bytes 393248 | tf_op jit(solution)/shard_map/ppermute | solution.py:63
  58.7 4.8 %all-to-all-start.1 = ((bf16[8,128,384]{2,1,0:T(8,128)(2,1)}), bf16[8,128,384]{2,1,0:T(8,128)(2,1)S(1)}, u32[]{:S(2)}, u32[]{:S(2)}) async-start(bf16[8,128,384]{2,1,0:T(8,128)(2,1)} %pack_q.1), calls=%async_computation.1 | async-start | bytes 1572864 | tf_op jit(solution)/shard_map/all_to_all | solution.py:732
  69.3 4.5 %collective-permute-done.13 = bf16[512,256]{1,0:T(8,128)(2,1)} collective-permute-done((bf16[512,256]{1,0:T(8,128)(2,1)S(1)}, bf16[512,256]{1,0:T(8,128)(2,1)}, u32[]{:S(2)}, u32[]{:S(2)}) %collective-permute-start.13) | collective-permute-done | bytes 262176 | tf_op jit(solution)/shard_map/ppermute | solution.py:55
  75.8 3.8 %broadcast_in_dim.11 = bf16[16,384,384]{2,1,0:T(8,128)(2,1)} broadcast(bf16[384,384]{1,0:T(8,128)(2,1)} %param.18), dimensions={1,2} | broadcast | bytes 5013504 | tf_op jit(solution)/shard_map/broadcast_in_dim | solution.py:730
  79.6 5.6 %all-to-all-start = ((bf16[16,384,384]{2,1,0:T(8,128)(2,1)}), bf16[16,384,384]{2,1,0:T(8,128)(2,1)}, u32[]{:S(2)}, u32[]{:S(2)}) async-start(bf16[16,384,384]{2,1,0:T(8,128)(2,1)} %broadcast_in_dim.11), calls=%async_computation | async-start | bytes 9437184 | tf_op jit(solution)/shard_map/all_to_all | solution.py:767
  87.2 44.9 %attention.1 = bf16[2,512,384]{2,1,0:T(8,128)(2,1)S(1)} custom-call(s32[53]{0:T(128)S(1)} %pad_add_fusion.4.items, s32[4,256]{1,0:T(4,128)S(1)} %pad_add_fusion.kpos_ref, bf16[8,128,384]{2,1,0:T(8,128)(2,1)S(1)} %all-to-all-done.1.q_ref, bf16[4,256,256]{2,1,0:T(8,128)(2,1)S(1)} %bitcast.39, bf16[4,256,256]{2,1,0:T(8,128)(2,1)S(1)} %bitcast.41, ...), custom_call_target="tpu_custom_call" | custom-call | flops 27000000512 | bytes 10000000 | tf_op jit(solution)/shard_map/attention/pallas_call | solution.py:272
  134.2 5.2 %collective-permute-start.34 = (bf16[512,384]{1,0:T(8,128)(2,1)S(1)}, bf16[512,384]{1,0:T(8,128)(2,1)S(1)}, u32[]{:S(2)}, u32[]{:S(2)}) collective-permute-start(bf16[512,384]{1,0:T(8,128)(2,1)S(1)} %get-tuple-element.18), channel_id=1, source_target_pairs={{0,120},{8,112},{16,104},{24,96},{32,88},{40,80},{48,72},{56,64},{... | collective-permute-start | bytes 1179656 | tf_op jit(solution)/shard_map/ppermute | solution.py:63
  139.4 3.9 %collective-permute-done.25.refs_1_ = bf16[512,384]{1,0:T(8,128)(2,1)S(1)} collective-permute-done((bf16[512,384]{1,0:T(8,128)(2,1)S(1)}, bf16[512,384]{1,0:T(8,128)(2,1)S(1)}, u32[]{:S(2)}, u32[]{:S(2)}) %collective-permute-start.25) | collective-permute-done | bytes 393248 | tf_op jit(solution)/shard_map/ppermute | solution.py:55
  146.1 7.9 %collective-permute-done.34.refs_0_ = bf16[512,384]{1,0:T(8,128)(2,1)S(1)} collective-permute-done((bf16[512,384]{1,0:T(8,128)(2,1)S(1)}, bf16[512,384]{1,0:T(8,128)(2,1)S(1)}, u32[]{:S(2)}, u32[]{:S(2)}) %collective-permute-start.34) | collective-permute-done | bytes 393248 | tf_op jit(solution)/shard_map/ppermute | solution.py:63
  156.6 8.1 %collective-permute-done.35.refs_1_ = bf16[512,384]{1,0:T(8,128)(2,1)S(1)} collective-permute-done((bf16[512,384]{1,0:T(8,128)(2,1)S(1)}, bf16[512,384]{1,0:T(8,128)(2,1)S(1)}, u32[]{:S(2)}, u32[]{:S(2)}) %collective-permute-start.35) | collective-permute-done | bytes 393248 | tf_op jit(solution)/shard_map/ppermute | solution.py:55
  171.1 3.8 %collective-permute-done.37.refs_3_ = bf16[256,384]{1,0:T(8,128)(2,1)S(1)} collective-permute-done((bf16[256,384]{1,0:T(8,128)(2,1)S(1)}, bf16[256,384]{1,0:T(8,128)(2,1)S(1)}, u32[]{:S(2)}, u32[]{:S(2)}) %collective-permute-start.37) | collective-permute-done | bytes 196640 | tf_op jit(solution)/shard_map/ppermute | solution.py:55
  182.2 6.1 %projection.2 = (bf16[8,128,768]{2,1,0:T(8,128)(2,1)S(1)}, bf16[3072,768]{1,0:T(8,128)(2,1)S(1)}) custom-call(s32[8]{0:T(128)S(1)} %pad_add_fusion.2.groups, bf16[8,2,384,384]{3,2,1,0:T(8,128)(2,1)} %bitcast.5.w_ref, bf16[512,384]{1,0:T(8,128)(2,1)S(1)} %get-tuple-element.19.refs_0_, bf16[512,384]{1,0:T(8,128)(2,1)S(1)} %copy-done.7, ...), custom_call_target="tpu_custom_call" | custom-call | flops 2500000000 | bytes 9000000 | tf_op jit(solution)/shard_map/projection/pallas_call | solution.py:341
  188.4 4.1 %projection.3 = bf16[8,128,768]{2,1,0:T(8,128)(2,1)S(1)} custom-call(s32[8]{0:T(128)S(1)} %pad_add_fusion.2.groups, bf16[3072,768]{1,0:T(8,128)(2,1)S(1)} %get-tuple-element.9.w_ref, bf16[512,384]{1,0:T(8,128)(2,1)S(1)} %collective-permute-done.34.refs_0_, bf16[512,384]{1,0:T(8,128)(2,1)S(1)} %collective-permute-done.35.refs_1_, ...), custom_call_target="tpu_custom_call", output_to_operand_aliasing={{}: (12, {})} | custom-call | flops 2500000000 | bytes 9000000 | tf_op jit(solution)/shard_map/projection/pallas_call | solution.py:341
  193.6 5.9 %all-to-all-start.3 = ((bf16[8,128,768]{2,1,0:T(8,128)(2,1)}), bf16[8,128,768]{2,1,0:T(8,128)(2,1)S(1)}, u32[]{:S(2)}, u32[]{:S(2)}) async-start(bf16[8,128,768]{2,1,0:T(8,128)(2,1)} %copy-done.1), calls=%async_computation.3 | async-start | bytes 3145728 | tf_op jit(solution)/shard_map/all_to_all | solution.py:778
  200.2 19.4 %all-to-all-done.3.update_ref = bf16[8,128,768]{2,1,0:T(8,128)(2,1)S(1)} async-done(((bf16[8,128,768]{2,1,0:T(8,128)(2,1)}), bf16[8,128,768]{2,1,0:T(8,128)(2,1)S(1)}, u32[]{:S(2)}, u32[]{:S(2)}) %all-to-all-start.3) | async-done | bytes 1572896 | tf_op jit(solution)/shard_map/all_to_all | solution.py:778
  219.6 5.2 %dispatch.1 = (bf16[16,264,384]{2,1,0:T(8,128)(2,1)S(1)}, f32[320,128]{1,0:T(8,128)S(1)}) custom-call(s32[2,128]{1,0:T(2,128)S(1)} %bitcast.45, bf16[8,128,768]{2,1,0:T(8,128)(2,1)S(1)} %all-to-all-done.3.update_ref, bf16[128,6144]{1,0:T(8,128)(2,1)S(1)} %copy-done, bf16[1,6144]{1,0:T(2,128)(2,1)S(1)} %reshape.644.gain_ref, bf16[8,6144]{1,0:T(8,128)(2,1)S(1)} %bitcast.44), custom_call_target="tpu_custom_call" | custom-call | flops 800000000 | bytes 8000000 | tf_op jit(solution)/shard_map/dispatch/pallas_call | solution.py:445
  224.8 43.2 %all_to_all.31.rows_ref = bf16[16,264,384]{2,1,0:T(8,128)(2,1)} all-to-all(bf16[16,264,384]{2,1,0:T(8,128)(2,1)S(1)} %get-tuple-element.12), channel_id=1, replica_groups=mesh['zh'=2,'x'=4,'zl'=2,'y'=4,'c'=2] {'zl','y','c'}, dimensions={0} | all-to-all | bytes 6488064 | tf_op jit(solution)/shard_map/all_to_all | solution.py:782
  268.0 7.2 %first_factor.1.own_ref = bf16[528,1024]{1,0:T(8,128)(2,1)} custom-call(bf16[16,264,384]{2,1,0:T(8,128)(2,1)} %all_to_all.31.rows_ref, bf16[1,3072,1024]{2,1,0:T(8,128)(2,1)} %u_ref.2), custom_call_target="tpu_custom_call" | custom-call | flops 3400000000 | bytes 9000000 | tf_op jit(solution)/shard_map/first_factor/pallas_call | solution.py:523
  278.3 12.9 %middle.1.own_ref = bf16[528,512]{1,0:T(8,128)(2,1)} custom-call(bf16[528,1024]{1,0:T(8,128)(2,1)} %first_factor.1.own_ref, bf16[528,1024]{1,0:T(8,128)(2,1)} %collective-permute-done.44.got_ref, bf16[1,2,512,4096]{3,2,1,0:T(8,128)(2,1)} %v_ref.2, bf16[1,4096,512]{2,1,0:T(8,128)(2,1)} %u_ref.3), custom_call_target="tpu_custom_call" | custom-call | flops 6700000256 | bytes 14000000 | tf_op jit(solution)/shard_map/middle/pallas_call | solution.py:588
  296.4 4.9 %last_factor.1 = bf16[16,264,384]{2,1,0:T(8,128)(2,1)S(1)} custom-call(bf16[528,512]{1,0:T(8,128)(2,1)S(1)} %copy-done.3, bf16[528,512]{1,0:T(8,128)(2,1)S(1)} %collective-permute-done.45.got_ref, bf16[1,512,3072]{2,1,0:T(8,128)(2,1)S(1)} %copy-done.2), custom_call_target="tpu_custom_call" | custom-call | flops 1700000000 | bytes 6000000 | tf_op jit(solution)/shard_map/last_factor/pallas_call | solution.py:643
  301.3 42.4 %all_to_all.32.back_ref = bf16[16,264,384]{2,1,0:T(8,128)(2,1)S(1)} all-to-all(bf16[16,264,384]{2,1,0:T(8,128)(2,1)S(1)} %last_factor.1), channel_id=1, replica_groups=mesh['zh'=2,'x'=4,'zl'=2,'y'=4,'c'=2] {'zl','y','c'}, dimensions={0} | all-to-all | bytes 6488064 | tf_op jit(solution)/shard_map/all_to_all | solution.py:786
  343.7 5.8 %combine.1 = bf16[128,6144]{1,0:T(8,128)(2,1)} custom-call(f32[320,128]{1,0:T(8,128)S(1)} %get-tuple-element.11.mix_ref, bf16[8,128,768]{2,1,0:T(8,128)(2,1)S(1)} %all-to-all-done.3.update_ref, bf16[128,6144]{1,0:T(8,128)(2,1)S(1)} %copy-done, bf16[16,264,384]{2,1,0:T(8,128)(2,1)S(1)} %all_to_all.32.back_ref), custom_call_target="tpu_custom_call" | custom-call | flops 1000000000 | bytes 8000000 | tf_op jit(solution)/shard_map/combine/pallas_call | solution.py:694
  (158 shorter events, 74.5 us)
Async XLA Ops:
  22.7 21.9 %collective-permute-start.4 = (bf16[1024,256]{1,0:T(8,128)(2,1)S(1)}, bf16[1024,256]{1,0:T(8,128)(2,1)S(1)}, u32[]{:S(2)}, u32[]{:S(2)}) collective-permute-start(bf16[1024,256]{1,0:T(8,128)(2,1)S(1)} %pad_maximum_fusion), channel_id=1, source_target_pairs={{0,16},{16,32},{32,48},{48,0},{1,17},{17,33},{33,49},{49,1},{2,18}... | collective-permute-start | bytes 1572872 | tf_op jit(solution)/shard_map/ppermute | solution.py:55
  24.3 16.7 %collective-permute-start.10 = (bf16[256,256]{1,0:T(8,128)(2,1)S(1)}, bf16[256,256]{1,0:T(8,128)(2,1)S(1)}, u32[]{:S(2)}, u32[]{:S(2)}) collective-permute-start(bf16[256,256]{1,0:T(8,128)(2,1)S(1)} %bitcast.46), channel_id=1, source_target_pairs={{0,32},{16,48},{32,0},{48,16},{1,33},{17,49},{33,1},{49,17},{2,34}... | collective-permute-start | bytes 393224 | tf_op jit(solution)/shard_map/ppermute | solution.py:55
  27.0 14.3 %collective-permute-start.8 = (bf16[256,256]{1,0:T(8,128)(2,1)S(1)}, bf16[256,256]{1,0:T(8,128)(2,1)S(1)}, u32[]{:S(2)}, u32[]{:S(2)}) collective-permute-start(bf16[256,256]{1,0:T(8,128)(2,1)S(1)} %bitcast.47), channel_id=1, source_target_pairs={{0,16},{16,32},{32,48},{48,0},{1,17},{17,33},{33,49},{49,1},{2,18}... | collective-permute-start | bytes 393224 | tf_op jit(solution)/shard_map/ppermute | solution.py:55
  27.0 14.3 %collective-permute-start.9 = (bf16[256,256]{1,0:T(8,128)(2,1)S(1)}, bf16[256,256]{1,0:T(8,128)(2,1)S(1)}, u32[]{:S(2)}, u32[]{:S(2)}) collective-permute-start(bf16[256,256]{1,0:T(8,128)(2,1)S(1)} %bitcast.48), channel_id=1, source_target_pairs={{0,48},{16,0},{32,16},{48,32},{1,49},{17,1},{33,17},{49,33},{2,50}... | collective-permute-start | bytes 393224 | tf_op jit(solution)/shard_map/ppermute | solution.py:55
  30.3 15.1 %collective-permute-start.5 = (bf16[1024,256]{1,0:T(8,128)(2,1)S(1)}, bf16[1024,256]{1,0:T(8,128)(2,1)S(1)}, u32[]{:S(2)}, u32[]{:S(2)}) collective-permute-start(bf16[1024,256]{1,0:T(8,128)(2,1)S(1)} %pad_maximum_fusion), channel_id=1, source_target_pairs={{0,48},{16,0},{32,16},{48,32},{1,49},{17,1},{33,17},{49,33},{2,50}... | collective-permute-start | bytes 1572872 | tf_op jit(solution)/shard_map/ppermute | solution.py:55
  41.0 12.7 %collective-permute-start = (bf16[64,3072]{1,0:T(8,128)(2,1)}, bf16[64,3072]{1,0:T(8,128)(2,1)}, u32[]{:S(2)}, u32[]{:S(2)}) collective-permute-start(bf16[64,3072]{1,0:T(8,128)(2,1)} %slice.45), channel_id=1, source_target_pairs={{0,120},{8,112},{16,104},{24,96},{32,88},{40,80},{48,72},{56,64},{... | collective-permute-start | bytes 1179656 | tf_op jit(solution)/shard_map/ppermute | solution.py:63
  41.3 22.2 %collective-permute-start.11 = (bf16[1024,256]{1,0:T(8,128)(2,1)S(1)}, bf16[1024,256]{1,0:T(8,128)(2,1)S(1)}, u32[]{:S(2)}, u32[]{:S(2)}) collective-permute-start(bf16[1024,256]{1,0:T(8,128)(2,1)S(1)} %pad_maximum_fusion.1), channel_id=1, source_target_pairs={{0,8},{8,64},{64,72},{72,0},{1,9},{9,65},{65,73},{73,1},{2,10},{10... | collective-permute-start | bytes 1572872 | tf_op jit(solution)/shard_map/ppermute | solution.py:55
  41.7 22.1 %collective-permute-start.12 = (bf16[1024,256]{1,0:T(8,128)(2,1)S(1)}, bf16[1024,256]{1,0:T(8,128)(2,1)}, u32[]{:S(2)}, u32[]{:S(2)}) collective-permute-start(bf16[1024,256]{1,0:T(8,128)(2,1)S(1)} %pad_maximum_fusion.1), channel_id=1, source_target_pairs={{0,72},{8,0},{64,8},{72,64},{1,73},{9,1},{65,9},{73,65},{2,74},{10... | collective-permute-start | bytes 1572872 | tf_op jit(solution)/shard_map/ppermute | solution.py:55
  44.6 20.9 %collective-permute-start.15 = (bf16[1024,256]{1,0:T(8,128)(2,1)S(1)}, bf16[1024,256]{1,0:T(8,128)(2,1)}, u32[]{:S(2)}, u32[]{:S(2)}) collective-permute-start(bf16[1024,256]{1,0:T(8,128)(2,1)S(1)} %pad_maximum_fusion), channel_id=1, source_target_pairs={{0,1},{1,0},{2,3},{3,2},{4,5},{5,4},{6,7},{7,6},{8,9},{9,8},{10,11... | collective-permute-start | bytes 1572872 | tf_op jit(solution)/shard_map/ppermute | solution.py:59
  45.4 23.4 %collective-permute-start.6 = (bf16[512,256]{1,0:T(8,128)(2,1)}, bf16[512,256]{1,0:T(8,128)(2,1)}, u32[]{:S(2)}, u32[]{:S(2)}) collective-permute-start(bf16[512,256]{1,0:T(8,128)(2,1)} %slice.61), channel_id=1, source_target_pairs={{0,16},{16,32},{32,48},{48,0},{1,17},{17,33},{33,49},{49,1},{2,18}... | collective-permute-start | bytes 786440 | tf_op jit(solution)/shard_map/ppermute | solution.py:55
  53.7 15.1 %collective-permute-start.7 = (bf16[512,256]{1,0:T(8,128)(2,1)}, bf16[512,256]{1,0:T(8,128)(2,1)}, u32[]{:S(2)}, u32[]{:S(2)}) collective-permute-start(bf16[512,256]{1,0:T(8,128)(2,1)} %slice.62), channel_id=1, source_target_pairs={{0,48},{16,0},{32,16},{48,32},{1,49},{17,1},{33,17},{49,33},{2,50}... | collective-permute-start | bytes 786440 | tf_op jit(solution)/shard_map/ppermute | solution.py:55
  58.7 17.1 %all-to-all-start.1 = ((bf16[8,128,384]{2,1,0:T(8,128)(2,1)}), bf16[8,128,384]{2,1,0:T(8,128)(2,1)S(1)}, u32[]{:S(2)}, u32[]{:S(2)}) async-start(bf16[8,128,384]{2,1,0:T(8,128)(2,1)} %pack_q.1), calls=%async_computation.1 | async-start | bytes 1572864 | tf_op jit(solution)/shard_map/all_to_all | solution.py:732
  73.9 13.3 %collective-permute-start.16 = (bf16[1024,256]{1,0:T(8,128)(2,1)S(1)}, bf16[1024,256]{1,0:T(8,128)(2,1)}, u32[]{:S(2)}, u32[]{:S(2)}) collective-permute-start(bf16[1024,256]{1,0:T(8,128)(2,1)S(1)} %collective-permute-done.4), channel_id=1, source_target_pairs={{0,1},{1,0},{2,3},{3,2},{4,5},{5,4},{6,7},{7,6},{8,9},{9,8},{10,11... | collective-permute-start | bytes 1572872 | tf_op jit(solution)/shard_map/ppermute | solution.py:59
  75.0 12.2 %collective-permute-start.17 = (bf16[1024,256]{1,0:T(8,128)(2,1)S(1)}, bf16[1024,256]{1,0:T(8,128)(2,1)}, u32[]{:S(2)}, u32[]{:S(2)}) collective-permute-start(bf16[1024,256]{1,0:T(8,128)(2,1)S(1)} %collective-permute-done.5), channel_id=1, source_target_pairs={{0,1},{1,0},{2,3},{3,2},{4,5},{5,4},{6,7},{7,6},{8,9},{9,8},{10,11... | collective-permute-start | bytes 1572872 | tf_op jit(solution)/shard_map/ppermute | solution.py:59
  75.0 12.2 %collective-permute-start.21 = (bf16[1024,256]{1,0:T(8,128)(2,1)S(1)}, bf16[1024,256]{1,0:T(8,128)(2,1)}, u32[]{:S(2)}, u32[]{:S(2)}) collective-permute-start(bf16[1024,256]{1,0:T(8,128)(2,1)S(1)} %collective-permute-done.11), channel_id=1, source_target_pairs={{0,1},{1,0},{2,3},{3,2},{4,5},{5,4},{6,7},{7,6},{8,9},{9,8},{10,11... | collective-permute-start | bytes 1572872 | tf_op jit(solution)/shard_map/ppermute | solution.py:59
  79.6 97.7 %all-to-all-start = ((bf16[16,384,384]{2,1,0:T(8,128)(2,1)}), bf16[16,384,384]{2,1,0:T(8,128)(2,1)}, u32[]{:S(2)}, u32[]{:S(2)}) async-start(bf16[16,384,384]{2,1,0:T(8,128)(2,1)} %broadcast_in_dim.11), calls=%async_computation | async-start | bytes 9437184 | tf_op jit(solution)/shard_map/all_to_all | solution.py:767
  134.2 19.8 %collective-permute-start.34 = (bf16[512,384]{1,0:T(8,128)(2,1)S(1)}, bf16[512,384]{1,0:T(8,128)(2,1)S(1)}, u32[]{:S(2)}, u32[]{:S(2)}) collective-permute-start(bf16[512,384]{1,0:T(8,128)(2,1)S(1)} %get-tuple-element.18), channel_id=1, source_target_pairs={{0,120},{8,112},{16,104},{24,96},{32,88},{40,80},{48,72},{56,64},{... | collective-permute-start | bytes 1179656 | tf_op jit(solution)/shard_map/ppermute | solution.py:63
  143.4 12.6 %collective-permute-start.27 = (bf16[256,384]{1,0:T(8,128)(2,1)S(1)}, bf16[256,384]{1,0:T(8,128)(2,1)}, u32[]{:S(2)}, u32[]{:S(2)}) collective-permute-start(bf16[256,384]{1,0:T(8,128)(2,1)S(1)} %slice.67), channel_id=1, source_target_pairs={{0,2},{2,4},{4,6},{6,0},{1,3},{3,5},{5,7},{7,1},{8,10},{10,12},{12... | collective-permute-start | bytes 589832 | tf_op jit(solution)/shard_map/ppermute | solution.py:55
  156.6 12.3 %collective-permute-start.31 = (bf16[512,384]{1,0:T(8,128)(2,1)S(1)}, bf16[512,384]{1,0:T(8,128)(2,1)S(1)}, u32[]{:S(2)}, u32[]{:S(2)}) collective-permute-start(bf16[512,384]{1,0:T(8,128)(2,1)S(1)} %collective-permute-done.26.refs_2_), channel_id=1, source_target_pairs={{0,1},{1,0},{2,3},{3,2},{4,5},{5,4},{6,7},{7,6},{8,9},{9,8},{10,11... | collective-permute-start | bytes 1179656 | tf_op jit(solution)/shard_map/ppermute | solution.py:59
  166.4 21.9 %collective-permute-start.39 = (bf16[512,384]{1,0:T(8,128)(2,1)S(1)}, bf16[512,384]{1,0:T(8,128)(2,1)S(1)}, u32[]{:S(2)}, u32[]{:S(2)}) collective-permute-start(bf16[512,384]{1,0:T(8,128)(2,1)S(1)} %collective-permute-done.34.refs_0_), channel_id=1, source_target_pairs={{0,1},{1,0},{2,3},{3,2},{4,5},{5,4},{6,7},{7,6},{8,9},{9,8},{10,11... | collective-permute-start | bytes 1179656 | tf_op jit(solution)/shard_map/ppermute | solution.py:59
  170.5 17.9 %collective-permute-start.40 = (bf16[512,384]{1,0:T(8,128)(2,1)S(1)}, bf16[512,384]{1,0:T(8,128)(2,1)S(1)}, u32[]{:S(2)}, u32[]{:S(2)}) collective-permute-start(bf16[512,384]{1,0:T(8,128)(2,1)S(1)} %collective-permute-done.35.refs_1_), channel_id=1, source_target_pairs={{0,1},{1,0},{2,3},{3,2},{4,5},{5,4},{6,7},{7,6},{8,9},{9,8},{10,11... | collective-permute-start | bytes 1179656 | tf_op jit(solution)/shard_map/ppermute | solution.py:59
  170.5 17.8 %collective-permute-start.41 = (bf16[512,384]{1,0:T(8,128)(2,1)S(1)}, bf16[512,384]{1,0:T(8,128)(2,1)S(1)}, u32[]{:S(2)}, u32[]{:S(2)}) collective-permute-start(bf16[512,384]{1,0:T(8,128)(2,1)S(1)} %collective-permute-done.36.refs_2_), channel_id=1, source_target_pairs={{0,1},{1,0},{2,3},{3,2},{4,5},{5,4},{6,7},{7,6},{8,9},{9,8},{10,11... | collective-permute-start | bytes 1179656 | tf_op jit(solution)/shard_map/ppermute | solution.py:59
  174.9 13.4 %collective-permute-start.42 = (bf16[256,384]{1,0:T(8,128)(2,1)S(1)}, bf16[256,384]{1,0:T(8,128)(2,1)S(1)}, u32[]{:S(2)}, u32[]{:S(2)}) collective-permute-start(bf16[256,384]{1,0:T(8,128)(2,1)S(1)} %collective-permute-done.37.refs_3_), channel_id=1, source_target_pairs={{0,1},{1,0},{2,3},{3,2},{4,5},{5,4},{6,7},{7,6},{8,9},{9,8},{10,11... | collective-permute-start | bytes 589832 | tf_op jit(solution)/shard_map/ppermute | solution.py:59
  193.6 26.0 %all-to-all-start.3 = ((bf16[8,128,768]{2,1,0:T(8,128)(2,1)}), bf16[8,128,768]{2,1,0:T(8,128)(2,1)S(1)}, u32[]{:S(2)}, u32[]{:S(2)}) async-start(bf16[8,128,768]{2,1,0:T(8,128)(2,1)} %copy-done.1), calls=%async_computation.3 | async-start | bytes 3145728 | tf_op jit(solution)/shard_map/all_to_all | solution.py:778
  (45 other events, 392.5 us)
where the time goes:
time: 354 us; the launch traced here: 349 us
  blocking collectives  95.5 us (27%)
  Pallas kernels  93.2 us (26%)
  waiting for transfers between devices  78.2 us (22%)
  starting transfers between devices  59.7 us (17%)
  local copies, waits for them, and re-layouts  22 us (6%)
    pallas_call x1, Pallas kernels, attention(): pl.pallas_call(attention_kernel, out_shape=jax.ShapeDtypeStruct((2, Q_ROW...  44.9 us
    all_to_all x1, blocking collectives, per_device(): lax.all_to_all(send, EXP, split_axis=0, concat_axis=0, tiled=True)  43.2 us
    all_to_all x1, blocking collectives, per_device(): lax.all_to_all(out_rows, EXP, split_axis=0, concat_axis=0, tiled=True)  42.4 us
    ppermute x22, waiting for transfers between devices, shifted(): return lax.ppermute(value, axis, [(i, (i + step) % 4) for i in range(4)])  38.8 us
    ppermute x22, starting transfers between devices, shifted(): return lax.ppermute(value, axis, [(i, (i + step) % 4) for i in range(4)])  34.2 us
    all_to_all x1, waiting for transfers between devices, per_device(): lax.all_to_all(projected, GROUP, split_axis=0, concat_axis=0, tiled=True)  19.4 us
    ppermute x2, waiting for transfers between devices, mirrored(): return lax.ppermute(value, PLANE, [(i, 15 - i) for i in range(16)])  13.4 us
    unnamed x40, local copies, waits for them, and re-layouts  13.2 us
  transfers between devices with their start and end apart: 49, of which 18 were waited for; matrix products, arithmetic and copies ran while one was open for 3% of the time, Pallas kernels for 15%

commit v1 on v0

--- a/solution.py
+++ b/solution.py
@@ -22,6 +22,7 @@
 BLOCKS = 8
 BLOCK_WIDTH = HALF // BLOCKS
 SLOTS = 32
+UNROLL = 8
 PART = 16
 EPS = 1e-05
 SCALE = HEAD_DIM**-0.5 * 1.4426950408889634
@@ -107,7 +108,7 @@
         in_specs=[ANY] * len(sources),
         out_specs=VMEM,
         scratch_shapes=[pltpu.SemaphoreType.DMA((shape[0] * len(sources),))],
-        compiler_params=params(8),
+        compiler_params=params(63),
         cost_estimate=cost(1_000_000_000, 2_000_000),
         name="pack",
     )(*sources)
@@ -320,15 +321,14 @@
         copy.start()
     for copy in copies:
         copy.wait()
-    for tile in range(Q_ROWS // Q_TILE):
-        total = jnp.dot(
-            rows_ref[tile * Q_TILE : (tile + 1) * Q_TILE, :],
-            w_all[...],
-            preferred_element_type=jnp.float32,
-        )
-        done_ref[tile * SOURCES : (tile + 1) * SOURCES] = total.astype(jnp.bfloat16).reshape(
-            SOURCES, HALF_TOK, 2 * GROUP_WIDTH
-        )
+
+    def one_side(side, carry):
+        columns = pl.ds(pl.multiple_of(side * 256, 256), 256)
+        total = jnp.dot(rows_ref[...], w_all[:, columns], preferred_element_type=jnp.float32)
+        done_ref[:, :, columns] = total.astype(jnp.bfloat16).reshape(8, HALF_TOK, 256)
+        return carry
+
+    lax.fori_loop(0, 2 * GROUP_WIDTH // 256, one_side, 0)
     out = pltpu.make_async_copy(done_ref, out_ref.at[:, pl.ds(first, HALF_TOK), :], out_sem)
     out.start()
     out.wait()
@@ -416,7 +416,7 @@
             return tail_rows + jnp.dot(chosen, rows, preferred_element_type=jnp.float32)
 
         empty = jnp.zeros((EXPERTS * BLOCKS, BLOCK_WIDTH), jnp.float32)
-        tail_rows = lax.fori_loop(0, BLOCKS, one_block, empty)
+        tail_rows = lax.fori_loop(0, BLOCKS, one_block, empty, unroll=True)
         tail_rows = tail_rows.astype(jnp.bfloat16)
         for expert in range(EXPERTS):
             send_ref[2 * expert + half, BLOCKS * SLOTS :, :] = tail_rows[
@@ -510,13 +510,24 @@
             move.wait()
         copies[group].wait()
         rows = x_ref[:, :, at : at + GROUP_DEPTH].reshape(ALL_ROWS, GROUP_DEPTH)
-        term = jnp.dot(rows, w_ref[at : at + GROUP_DEPTH, :], preferred_element_type=jnp.float32)
-        if group == 0:
-            acc_ref[...] = term
-        elif group < GROUPS - 1:
-            acc_ref[...] += term
-        else:
-            low_ref[...] = (acc_ref[...] + term).astype(jnp.bfloat16)
+        acc = None if group == 0 else acc_ref
+
+        def one_tile(tile, carry, at=at, rows=rows, acc=acc, last=group == GROUPS - 1):
+            columns = pl.ds(pl.multiple_of(tile * RANK_TILE, RANK_TILE), RANK_TILE)
+            weights = w_ref[at : at + GROUP_DEPTH, columns]
+            term = jnp.dot(rows, weights, preferred_element_type=jnp.float32)
+            if acc is not None:
+                term = acc[:, columns] + term
+            if last:
+                low_ref[:, columns] = term.astype(jnp.bfloat16)
+            else:
+                acc_ref[:, columns] = term
+            return carry
+
+        lax.fori_loop(0, 2 * RANK // RANK_TILE, one_tile, 0)
+
+
+RANK_TILE = 512
 
 
 def first_factor(received, u_gate_up):
@@ -539,7 +550,7 @@
     )(received, u_gate_up)
 
 
-FF_TILE = 512
+FF_TILE = 1024
 FF_STEPS = FF_PIECE // FF_TILE
 
 
@@ -687,7 +698,7 @@
             out_ref[:, at] = (stream + mixture).astype(jnp.bfloat16)
             return carry
 
-        lax.fori_loop(0, BLOCKS, one_block, 0)
+        lax.fori_loop(0, BLOCKS, one_block, 0, unroll=UNROLL)
 
 
 def combine(mix, update, residual, back):

time: 354 us -> 352 us (level)
  Pallas kernels: 93.2 us -> 89.4 us
    unnamed x40 -> x52, local copies, waits for them, and re-layouts: 13.2 us -> 15.7 us
where the time goes in v1:
time: 352 us; the launch traced here: 347 us
  blocking collectives  95.7 us (27%)
  Pallas kernels  89.4 us (25%)
  waiting for transfers between devices  76.3 us (22%)
  starting transfers between devices  58.9 us (17%)
  local copies, waits for them, and re-layouts  25.5 us (7%)
    pallas_call x1, Pallas kernels, attention(): pl.pallas_call(attention_kernel, out_shape=jax.ShapeDtypeStruct((2, Q_ROW...  44.7 us
    all_to_all x1, blocking collectives, per_device(): lax.all_to_all(send, EXP, split_axis=0, concat_axis=0, tiled=True)  43.2 us
    all_to_all x1, blocking collectives, per_device(): lax.all_to_all(out_rows, EXP, split_axis=0, concat_axis=0, tiled=True)  42.4 us
    ppermute x22, waiting for transfers between devices, shifted(): return lax.ppermute(value, axis, [(i, (i + step) % 4) for i in range(4)])  38.5 us
    ppermute x22, starting transfers between devices, shifted(): return lax.ppermute(value, axis, [(i, (i + step) % 4) for i in range(4)])  33.9 us
    all_to_all x1, waiting for transfers between devices, per_device(): lax.all_to_all(projected, GROUP, split_axis=0, concat_axis=0, tiled=True)  19.4 us
    unnamed x52, local copies, waits for them, and re-layouts  15.7 us
    pallas_call x1, Pallas kernels, middle(): pl.pallas_call(middle_kernel, out_shape=jax.ShapeDtypeStruct((ALL_ROWS, R...  12.4 us
  transfers between devices with their start and end apart: 49, of which 18 were waited for; matrix products, arithmetic and copies ran while one was open for 3% of the time, Pallas kernels for 15%

profile of v1, /device:TPU:8, one launch (start us, length us, event | category | flops | bytes accessed | tf_op | source)
XLA Modules:
  0.0 346.7 jit_solution(14686611555313796150)
XLA Ops:
  1.7 10.1 %all_to_all.30 = bf16[4,128,256]{2,1,0:T(8,128)(2,1)S(1)} all-to-all(bf16[4,128,256]{2,1,0:T(8,128)(2,1)} %pack.1), channel_id=1, replica_groups=mesh['zh'=2,'x'=4,'zl'=2,'y'=4,'c'=2] {'y'}, dimensions={0} | all-to-all | bytes 524288 | tf_op jit(solution)/shard_map/all_to_all | solution.py:737
  27.0 3.2 collective-permute-start.9
  31.2 9.7 %collective-permute-done.10 = bf16[256,256]{1,0:T(8,128)(2,1)S(1)} collective-permute-done((bf16[256,256]{1,0:T(8,128)(2,1)S(1)}, bf16[256,256]{1,0:T(8,128)(2,1)S(1)}, u32[]{:S(2)}, u32[]{:S(2)}) %collective-permute-start.10) | collective-permute-done | bytes 131104 | tf_op jit(solution)/shard_map/ppermute | solution.py:56
  48.2 5.3 %collective-permute-done.far_ref = bf16[64,3072]{1,0:T(8,128)(2,1)S(1)} collective-permute-done((bf16[64,3072]{1,0:T(8,128)(2,1)}, bf16[64,3072]{1,0:T(8,128)(2,1)S(1)}, u32[]{:S(2)}, u32[]{:S(2)}) %collective-permute-start) | collective-permute-done | bytes 393248 | tf_op jit(solution)/shard_map/ppermute | solution.py:64
  59.4 4.8 %all-to-all-start.1 = ((bf16[8,128,384]{2,1,0:T(8,128)(2,1)}), bf16[8,128,384]{2,1,0:T(8,128)(2,1)S(1)}, u32[]{:S(2)}, u32[]{:S(2)}) async-start(bf16[8,128,384]{2,1,0:T(8,128)(2,1)} %pack_q.1), calls=%async_computation.1 | async-start | bytes 1572864 | tf_op jit(solution)/shard_map/all_to_all | solution.py:743
  71.0 4.5 %collective-permute-done.13 = bf16[512,256]{1,0:T(8,128)(2,1)} collective-permute-done((bf16[512,256]{1,0:T(8,128)(2,1)S(1)}, bf16[512,256]{1,0:T(8,128)(2,1)}, u32[]{:S(2)}, u32[]{:S(2)}) %collective-permute-start.13) | collective-permute-done | bytes 262176 | tf_op jit(solution)/shard_map/ppermute | solution.py:56
  78.1 3.8 %broadcast_in_dim.11 = bf16[16,384,384]{2,1,0:T(8,128)(2,1)} broadcast(bf16[384,384]{1,0:T(8,128)(2,1)} %param.18), dimensions={1,2} | broadcast | bytes 5013504 | tf_op jit(solution)/shard_map/broadcast_in_dim | solution.py:741
  81.9 5.1 %all-to-all-start = ((bf16[16,384,384]{2,1,0:T(8,128)(2,1)}), bf16[16,384,384]{2,1,0:T(8,128)(2,1)}, u32[]{:S(2)}, u32[]{:S(2)}) async-start(bf16[16,384,384]{2,1,0:T(8,128)(2,1)} %broadcast_in_dim.11), calls=%async_computation | async-start | bytes 9437184 | tf_op jit(solution)/shard_map/all_to_all | solution.py:778
  91.0 44.7 %attention.1 = bf16[2,512,384]{2,1,0:T(8,128)(2,1)S(1)} custom-call(s32[53]{0:T(128)S(1)} %pad_add_fusion.4.items, s32[4,256]{1,0:T(4,128)S(1)} %pad_add_fusion.kpos_ref, bf16[8,128,384]{2,1,0:T(8,128)(2,1)S(1)} %all-to-all-done.1.q_ref, bf16[4,256,256]{2,1,0:T(8,128)(2,1)S(1)} %bitcast.39, bf16[4,256,256]{2,1,0:T(8,128)(2,1)S(1)} %bitcast.41, ...), custom_call_target="tpu_custom_call" | custom-call | flops 27000000512 | bytes 10000000 | tf_op jit(solution)/shard_map/attention/pallas_call | solution.py:273
  137.9 5.2 %collective-permute-start.34 = (bf16[512,384]{1,0:T(8,128)(2,1)S(1)}, bf16[512,384]{1,0:T(8,128)(2,1)S(1)}, u32[]{:S(2)}, u32[]{:S(2)}) collective-permute-start(bf16[512,384]{1,0:T(8,128)(2,1)S(1)} %get-tuple-element.18), channel_id=1, source_target_pairs={{0,120},{8,112},{16,104},{24,96},{32,88},{40,80},{48,72},{56,64},{... | collective-permute-start | bytes 1179656 | tf_op jit(solution)/shard_map/ppermute | solution.py:64
  143.1 4.0 %collective-permute-done.25.refs_1_ = bf16[512,384]{1,0:T(8,128)(2,1)S(1)} collective-permute-done((bf16[512,384]{1,0:T(8,128)(2,1)S(1)}, bf16[512,384]{1,0:T(8,128)(2,1)S(1)}, u32[]{:S(2)}, u32[]{:S(2)}) %collective-permute-start.25) | collective-permute-done | bytes 393248 | tf_op jit(solution)/shard_map/ppermute | solution.py:56
  149.4 6.5 %collective-permute-done.34.refs_0_ = bf16[512,384]{1,0:T(8,128)(2,1)S(1)} collective-permute-done((bf16[512,384]{1,0:T(8,128)(2,1)S(1)}, bf16[512,384]{1,0:T(8,128)(2,1)S(1)}, u32[]{:S(2)}, u32[]{:S(2)}) %collective-permute-start.34) | collective-permute-done | bytes 393248 | tf_op jit(solution)/shard_map/ppermute | solution.py:64
  158.5 8.1 %collective-permute-done.35.refs_1_ = bf16[512,384]{1,0:T(8,128)(2,1)S(1)} collective-permute-done((bf16[512,384]{1,0:T(8,128)(2,1)S(1)}, bf16[512,384]{1,0:T(8,128)(2,1)S(1)}, u32[]{:S(2)}, u32[]{:S(2)}) %collective-permute-start.35) | collective-permute-done | bytes 393248 | tf_op jit(solution)/shard_map/ppermute | solution.py:56
  173.4 3.4 collective-permute-done.37.refs_3_
  183.8 6.4 %projection.2 = (bf16[8,128,768]{2,1,0:T(8,128)(2,1)S(1)}, bf16[3072,768]{1,0:T(8,128)(2,1)S(1)}) custom-call(s32[8]{0:T(128)S(1)} %pad_add_fusion.2.groups, bf16[8,2,384,384]{3,2,1,0:T(8,128)(2,1)} %bitcast.5.w_ref, bf16[512,384]{1,0:T(8,128)(2,1)S(1)} %get-tuple-element.19.refs_0_, bf16[512,384]{1,0:T(8,128)(2,1)S(1)} %copy-done.9, ...), custom_call_target="tpu_custom_call" | custom-call | flops 2500000000 | bytes 9000000 | tf_op jit(solution)/shard_map/projection/pallas_call | solution.py:341
  190.3 4.4 %projection.3 = bf16[8,128,768]{2,1,0:T(8,128)(2,1)S(1)} custom-call(s32[8]{0:T(128)S(1)} %pad_add_fusion.2.groups, bf16[3072,768]{1,0:T(8,128)(2,1)S(1)} %get-tuple-element.9.w_ref, bf16[512,384]{1,0:T(8,128)(2,1)S(1)} %collective-permute-done.34.refs_0_, bf16[512,384]{1,0:T(8,128)(2,1)S(1)} %collective-permute-done.35.refs_1_, ...), custom_call_target="tpu_custom_call", output_to_operand_aliasing={{}: (12, {})} | custom-call | flops 2500000000 | bytes 9000000 | tf_op jit(solution)/shard_map/projection/pallas_call | solution.py:341
  195.9 5.9 %all-to-all-start.3 = ((bf16[8,128,768]{2,1,0:T(8,128)(2,1)}), bf16[8,128,768]{2,1,0:T(8,128)(2,1)S(1)}, u32[]{:S(2)}, u32[]{:S(2)}) async-start(bf16[8,128,768]{2,1,0:T(8,128)(2,1)} %copy-done.1), calls=%async_computation.3 | async-start | bytes 3145728 | tf_op jit(solution)/shard_map/all_to_all | solution.py:789
  202.5 19.4 %all-to-all-done.3.update_ref = bf16[8,128,768]{2,1,0:T(8,128)(2,1)S(1)} async-done(((bf16[8,128,768]{2,1,0:T(8,128)(2,1)}), bf16[8,128,768]{2,1,0:T(8,128)(2,1)S(1)}, u32[]{:S(2)}, u32[]{:S(2)}) %all-to-all-start.3) | async-done | bytes 1572896 | tf_op jit(solution)/shard_map/all_to_all | solution.py:789
  224.3 43.2 %all_to_all.31.rows_ref = bf16[16,264,384]{2,1,0:T(8,128)(2,1)} all-to-all(bf16[16,264,384]{2,1,0:T(8,128)(2,1)S(1)} %get-tuple-element.12), channel_id=1, replica_groups=mesh['zh'=2,'x'=4,'zl'=2,'y'=4,'c'=2] {'zl','y','c'}, dimensions={0} | all-to-all | bytes 6488064 | tf_op jit(solution)/shard_map/all_to_all | solution.py:793
  267.4 7.9 %first_factor.1.own_ref = bf16[528,1024]{1,0:T(8,128)(2,1)} custom-call(bf16[16,264,384]{2,1,0:T(8,128)(2,1)} %all_to_all.31.rows_ref, bf16[1,3072,1024]{2,1,0:T(8,128)(2,1)} %u_ref.2), custom_call_target="tpu_custom_call" | custom-call | flops 3400000000 | bytes 9000000 | tf_op jit(solution)/shard_map/first_factor/pallas_call | solution.py:534
  278.5 12.4 %middle.1.own_ref = bf16[528,512]{1,0:T(8,128)(2,1)} custom-call(bf16[528,1024]{1,0:T(8,128)(2,1)} %first_factor.1.own_ref, bf16[528,1024]{1,0:T(8,128)(2,1)} %collective-permute-done.44.got_ref, bf16[1,2,512,4096]{3,2,1,0:T(8,128)(2,1)} %v_ref.2, bf16[1,4096,512]{2,1,0:T(8,128)(2,1)} %u_ref.3), custom_call_target="tpu_custom_call" | custom-call | flops 6700000256 | bytes 14000000 | tf_op jit(solution)/shard_map/middle/pallas_call | solution.py:599
  296.0 4.9 %last_factor.1 = bf16[16,264,384]{2,1,0:T(8,128)(2,1)S(1)} custom-call(bf16[528,512]{1,0:T(8,128)(2,1)S(1)} %copy-done.3, bf16[528,512]{1,0:T(8,128)(2,1)S(1)} %collective-permute-done.45.got_ref, bf16[1,512,3072]{2,1,0:T(8,128)(2,1)S(1)} %copy-done.2), custom_call_target="tpu_custom_call" | custom-call | flops 1700000000 | bytes 6000000 | tf_op jit(solution)/shard_map/last_factor/pallas_call | solution.py:654
  300.9 42.4 %all_to_all.32.back_ref = bf16[16,264,384]{2,1,0:T(8,128)(2,1)S(1)} all-to-all(bf16[16,264,384]{2,1,0:T(8,128)(2,1)S(1)} %last_factor.1), channel_id=1, replica_groups=mesh['zh'=2,'x'=4,'zl'=2,'y'=4,'c'=2] {'zl','y','c'}, dimensions={0} | all-to-all | bytes 6488064 | tf_op jit(solution)/shard_map/all_to_all | solution.py:797
  343.3 3.4 combine.1
  (170 shorter events, 77.6 us)
Async XLA Ops:
  22.7 21.9 %collective-permute-start.4 = (bf16[1024,256]{1,0:T(8,128)(2,1)S(1)}, bf16[1024,256]{1,0:T(8,128)(2,1)S(1)}, u32[]{:S(2)}, u32[]{:S(2)}) collective-permute-start(bf16[1024,256]{1,0:T(8,128)(2,1)S(1)} %pad_maximum_fusion), channel_id=1, source_target_pairs={{0,16},{16,32},{32,48},{48,0},{1,17},{17,33},{33,49},{49,1},{2,18}... | collective-permute-start | bytes 1572872 | tf_op jit(solution)/shard_map/ppermute | solution.py:56
  24.2 16.7 %collective-permute-start.10 = (bf16[256,256]{1,0:T(8,128)(2,1)S(1)}, bf16[256,256]{1,0:T(8,128)(2,1)S(1)}, u32[]{:S(2)}, u32[]{:S(2)}) collective-permute-start(bf16[256,256]{1,0:T(8,128)(2,1)S(1)} %bitcast.48), channel_id=1, source_target_pairs={{0,32},{16,48},{32,0},{48,16},{1,33},{17,49},{33,1},{49,17},{2,34}... | collective-permute-start | bytes 393224 | tf_op jit(solution)/shard_map/ppermute | solution.py:56
  26.9 14.3 %collective-permute-start.8 = (bf16[256,256]{1,0:T(8,128)(2,1)S(1)}, bf16[256,256]{1,0:T(8,128)(2,1)S(1)}, u32[]{:S(2)}, u32[]{:S(2)}) collective-permute-start(bf16[256,256]{1,0:T(8,128)(2,1)S(1)} %bitcast.49), channel_id=1, source_target_pairs={{0,16},{16,32},{32,48},{48,0},{1,17},{17,33},{33,49},{49,1},{2,18}... | collective-permute-start | bytes 393224 | tf_op jit(solution)/shard_map/ppermute | solution.py:56
  27.0 14.3 %collective-permute-start.9 = (bf16[256,256]{1,0:T(8,128)(2,1)S(1)}, bf16[256,256]{1,0:T(8,128)(2,1)S(1)}, u32[]{:S(2)}, u32[]{:S(2)}) collective-permute-start(bf16[256,256]{1,0:T(8,128)(2,1)S(1)} %bitcast.50), channel_id=1, source_target_pairs={{0,48},{16,0},{32,16},{48,32},{1,49},{17,1},{33,17},{49,33},{2,50}... | collective-permute-start | bytes 393224 | tf_op jit(solution)/shard_map/ppermute | solution.py:56
  30.2 15.1 %collective-permute-start.5 = (bf16[1024,256]{1,0:T(8,128)(2,1)S(1)}, bf16[1024,256]{1,0:T(8,128)(2,1)S(1)}, u32[]{:S(2)}, u32[]{:S(2)}) collective-permute-start(bf16[1024,256]{1,0:T(8,128)(2,1)S(1)} %pad_maximum_fusion), channel_id=1, source_target_pairs={{0,48},{16,0},{32,16},{48,32},{1,49},{17,1},{33,17},{49,33},{2,50}... | collective-permute-start | bytes 1572872 | tf_op jit(solution)/shard_map/ppermute | solution.py:56
  40.9 12.6 %collective-permute-start = (bf16[64,3072]{1,0:T(8,128)(2,1)}, bf16[64,3072]{1,0:T(8,128)(2,1)S(1)}, u32[]{:S(2)}, u32[]{:S(2)}) collective-permute-start(bf16[64,3072]{1,0:T(8,128)(2,1)} %slice.45), channel_id=1, source_target_pairs={{0,120},{8,112},{16,104},{24,96},{32,88},{40,80},{48,72},{56,64},{... | collective-permute-start | bytes 1179656 | tf_op jit(solution)/shard_map/ppermute | solution.py:64
  41.2 23.0 %collective-permute-start.11 = (bf16[1024,256]{1,0:T(8,128)(2,1)S(1)}, bf16[1024,256]{1,0:T(8,128)(2,1)}, u32[]{:S(2)}, u32[]{:S(2)}) collective-permute-start(bf16[1024,256]{1,0:T(8,128)(2,1)S(1)} %pad_maximum_fusion.1), channel_id=1, source_target_pairs={{0,8},{8,64},{64,72},{72,0},{1,9},{9,65},{65,73},{73,1},{2,10},{10... | collective-permute-start | bytes 1572872 | tf_op jit(solution)/shard_map/ppermute | solution.py:56
  41.6 23.9 %collective-permute-start.12 = (bf16[1024,256]{1,0:T(8,128)(2,1)S(1)}, bf16[1024,256]{1,0:T(8,128)(2,1)}, u32[]{:S(2)}, u32[]{:S(2)}) collective-permute-start(bf16[1024,256]{1,0:T(8,128)(2,1)S(1)} %pad_maximum_fusion.1), channel_id=1, source_target_pairs={{0,72},{8,0},{64,8},{72,64},{1,73},{9,1},{65,9},{73,65},{2,74},{10... | collective-permute-start | bytes 1572872 | tf_op jit(solution)/shard_map/ppermute | solution.py:56
  44.6 22.7 %collective-permute-start.15 = (bf16[1024,256]{1,0:T(8,128)(2,1)S(1)}, bf16[1024,256]{1,0:T(8,128)(2,1)}, u32[]{:S(2)}, u32[]{:S(2)}) collective-permute-start(bf16[1024,256]{1,0:T(8,128)(2,1)S(1)} %pad_maximum_fusion), channel_id=1, source_target_pairs={{0,1},{1,0},{2,3},{3,2},{4,5},{5,4},{6,7},{7,6},{8,9},{9,8},{10,11... | collective-permute-start | bytes 1572872 | tf_op jit(solution)/shard_map/ppermute | solution.py:60
  45.3 25.2 %collective-permute-start.6 = (bf16[512,256]{1,0:T(8,128)(2,1)}, bf16[512,256]{1,0:T(8,128)(2,1)}, u32[]{:S(2)}, u32[]{:S(2)}) collective-permute-start(bf16[512,256]{1,0:T(8,128)(2,1)} %slice.61), channel_id=1, source_target_pairs={{0,16},{16,32},{32,48},{48,0},{1,17},{17,33},{33,49},{49,1},{2,18}... | collective-permute-start | bytes 786440 | tf_op jit(solution)/shard_map/ppermute | solution.py:56
  54.2 16.2 %collective-permute-start.7 = (bf16[512,256]{1,0:T(8,128)(2,1)}, bf16[512,256]{1,0:T(8,128)(2,1)}, u32[]{:S(2)}, u32[]{:S(2)}) collective-permute-start(bf16[512,256]{1,0:T(8,128)(2,1)} %slice.62), channel_id=1, source_target_pairs={{0,48},{16,0},{32,16},{48,32},{1,49},{17,1},{33,17},{49,33},{2,50}... | collective-permute-start | bytes 786440 | tf_op jit(solution)/shard_map/ppermute | solution.py:56
  59.4 18.7 %all-to-all-start.1 = ((bf16[8,128,384]{2,1,0:T(8,128)(2,1)}), bf16[8,128,384]{2,1,0:T(8,128)(2,1)S(1)}, u32[]{:S(2)}, u32[]{:S(2)}) async-start(bf16[8,128,384]{2,1,0:T(8,128)(2,1)} %pack_q.1), calls=%async_computation.1 | async-start | bytes 1572864 | tf_op jit(solution)/shard_map/all_to_all | solution.py:743
  75.5 11.6 %collective-permute-start.23 = (bf16[512,256]{1,0:T(8,128)(2,1)}, bf16[512,256]{1,0:T(8,128)(2,1)}, u32[]{:S(2)}, u32[]{:S(2)}) collective-permute-start(bf16[512,256]{1,0:T(8,128)(2,1)} %collective-permute-done.13), channel_id=1, source_target_pairs={{0,1},{1,0},{2,3},{3,2},{4,5},{5,4},{6,7},{7,6},{8,9},{9,8},{10,11... | collective-permute-start | bytes 786440 | tf_op jit(solution)/shard_map/ppermute | solution.py:60
  75.6 13.5 %collective-permute-start.16 = (bf16[1024,256]{1,0:T(8,128)(2,1)S(1)}, bf16[1024,256]{1,0:T(8,128)(2,1)}, u32[]{:S(2)}, u32[]{:S(2)}) collective-permute-start(bf16[1024,256]{1,0:T(8,128)(2,1)S(1)} %collective-permute-done.4), channel_id=1, source_target_pairs={{0,1},{1,0},{2,3},{3,2},{4,5},{5,4},{6,7},{7,6},{8,9},{9,8},{10,11... | collective-permute-start | bytes 1572872 | tf_op jit(solution)/shard_map/ppermute | solution.py:60
  76.6 12.4 %collective-permute-start.17 = (bf16[1024,256]{1,0:T(8,128)(2,1)}, bf16[1024,256]{1,0:T(8,128)(2,1)}, u32[]{:S(2)}, u32[]{:S(2)}) collective-permute-start(bf16[1024,256]{1,0:T(8,128)(2,1)} %copy-done.5), channel_id=1, source_target_pairs={{0,1},{1,0},{2,3},{3,2},{4,5},{5,4},{6,7},{7,6},{8,9},{9,8},{10,11... | collective-permute-start | bytes 1572872 | tf_op jit(solution)/shard_map/ppermute | solution.py:60
  77.4 11.7 %collective-permute-start.21 = (bf16[1024,256]{1,0:T(8,128)(2,1)}, bf16[1024,256]{1,0:T(8,128)(2,1)}, u32[]{:S(2)}, u32[]{:S(2)}) collective-permute-start(bf16[1024,256]{1,0:T(8,128)(2,1)} %collective-permute-done.11), channel_id=1, source_target_pairs={{0,1},{1,0},{2,3},{3,2},{4,5},{5,4},{6,7},{7,6},{8,9},{9,8},{10,11... | collective-permute-start | bytes 1572872 | tf_op jit(solution)/shard_map/ppermute | solution.py:60
  81.9 96.9 %all-to-all-start = ((bf16[16,384,384]{2,1,0:T(8,128)(2,1)}), bf16[16,384,384]{2,1,0:T(8,128)(2,1)}, u32[]{:S(2)}, u32[]{:S(2)}) async-start(bf16[16,384,384]{2,1,0:T(8,128)(2,1)} %broadcast_in_dim.11), calls=%async_computation | async-start | bytes 9437184 | tf_op jit(solution)/shard_map/all_to_all | solution.py:778
  137.9 18.0 %collective-permute-start.34 = (bf16[512,384]{1,0:T(8,128)(2,1)S(1)}, bf16[512,384]{1,0:T(8,128)(2,1)S(1)}, u32[]{:S(2)}, u32[]{:S(2)}) collective-permute-start(bf16[512,384]{1,0:T(8,128)(2,1)S(1)} %get-tuple-element.18), channel_id=1, source_target_pairs={{0,120},{8,112},{16,104},{24,96},{32,88},{40,80},{48,72},{56,64},{... | collective-permute-start | bytes 1179656 | tf_op jit(solution)/shard_map/ppermute | solution.py:64
  158.4 12.7 %collective-permute-start.31 = (bf16[512,384]{1,0:T(8,128)(2,1)S(1)}, bf16[512,384]{1,0:T(8,128)(2,1)S(1)}, u32[]{:S(2)}, u32[]{:S(2)}) collective-permute-start(bf16[512,384]{1,0:T(8,128)(2,1)S(1)} %collective-permute-done.26.refs_2_), channel_id=1, source_target_pairs={{0,1},{1,0},{2,3},{3,2},{4,5},{5,4},{6,7},{7,6},{8,9},{9,8},{10,11... | collective-permute-start | bytes 1179656 | tf_op jit(solution)/shard_map/ppermute | solution.py:60
  168.7 21.6 %collective-permute-start.39 = (bf16[512,384]{1,0:T(8,128)(2,1)S(1)}, bf16[512,384]{1,0:T(8,128)(2,1)S(1)}, u32[]{:S(2)}, u32[]{:S(2)}) collective-permute-start(bf16[512,384]{1,0:T(8,128)(2,1)S(1)} %collective-permute-done.34.refs_0_), channel_id=1, source_target_pairs={{0,1},{1,0},{2,3},{3,2},{4,5},{5,4},{6,7},{7,6},{8,9},{9,8},{10,11... | collective-permute-start | bytes 1179656 | tf_op jit(solution)/shard_map/ppermute | solution.py:60
  172.8 17.5 %collective-permute-start.40 = (bf16[512,384]{1,0:T(8,128)(2,1)S(1)}, bf16[512,384]{1,0:T(8,128)(2,1)S(1)}, u32[]{:S(2)}, u32[]{:S(2)}) collective-permute-start(bf16[512,384]{1,0:T(8,128)(2,1)S(1)} %collective-permute-done.35.refs_1_), channel_id=1, source_target_pairs={{0,1},{1,0},{2,3},{3,2},{4,5},{5,4},{6,7},{7,6},{8,9},{9,8},{10,11... | collective-permute-start | bytes 1179656 | tf_op jit(solution)/shard_map/ppermute | solution.py:60
  172.8 17.5 %collective-permute-start.41 = (bf16[512,384]{1,0:T(8,128)(2,1)S(1)}, bf16[512,384]{1,0:T(8,128)(2,1)S(1)}, u32[]{:S(2)}, u32[]{:S(2)}) collective-permute-start(bf16[512,384]{1,0:T(8,128)(2,1)S(1)} %collective-permute-done.36.refs_2_), channel_id=1, source_target_pairs={{0,1},{1,0},{2,3},{3,2},{4,5},{5,4},{6,7},{7,6},{8,9},{9,8},{10,11... | collective-permute-start | bytes 1179656 | tf_op jit(solution)/shard_map/ppermute | solution.py:60
  176.8 13.5 %collective-permute-start.42 = (bf16[256,384]{1,0:T(8,128)(2,1)S(1)}, bf16[256,384]{1,0:T(8,128)(2,1)S(1)}, u32[]{:S(2)}, u32[]{:S(2)}) collective-permute-start(bf16[256,384]{1,0:T(8,128)(2,1)S(1)} %collective-permute-done.37.refs_3_), channel_id=1, source_target_pairs={{0,1},{1,0},{2,3},{3,2},{4,5},{5,4},{6,7},{7,6},{8,9},{9,8},{10,11... | collective-permute-start | bytes 589832 | tf_op jit(solution)/shard_map/ppermute | solution.py:60
  195.9 26.0 %all-to-all-start.3 = ((bf16[8,128,768]{2,1,0:T(8,128)(2,1)}), bf16[8,128,768]{2,1,0:T(8,128)(2,1)S(1)}, u32[]{:S(2)}, u32[]{:S(2)}) async-start(bf16[8,128,768]{2,1,0:T(8,128)(2,1)} %copy-done.1), calls=%async_computation.3 | async-start | bytes 3145728 | tf_op jit(solution)/shard_map/all_to_all | solution.py:789
  (51 other events, 397.8 us)
